TPU v7x, 32 devices: a whole 2x2x4 slice. The times are simulated.
32 devices in a mesh: dp: 32 (over z, y, x, core).
Axes of the slice: x: 2, y: 2, z: 4, core: 2. Of those that a mesh axis runs over, the one named last changes fastest.
Arguments:
- tokens: bfloat16 [32768, 768], P('dp'), may hold values from -6 to 6
- lengths: int32 [32], P('dp'), may hold values from 256 to 1024, as said below
- drops: int32 [32], P('dp'), may hold values 0 or 1
- cotangent: bfloat16 [32768, 768], P('dp'), may hold values from -6 to 6
- w_qkv: bfloat16 [768, 2304], P('dp'), may hold values from -0.3125 to 0.3125
- w_out: bfloat16 [768, 768], P('dp'), may hold values from -1.75 to 1.75
- w_up: bfloat16 [768, 3072], P('dp'), may hold values from -0.21875 to 0.21875
- w_down: bfloat16 [3072, 768], P('dp'), may hold values from -0.109375 to 0.109375
- attn_vectors: bfloat16 [768, 5], P('dp'), may hold values from 0.25 to 1.75
- ffn_vectors: bfloat16 [768, 3], P('dp'), may hold values from 0.25 to 1.75
- up_bias: bfloat16 [3072], P('dp'), may hold values from -3 to 3
Outputs:
- result: bfloat16 [32768, 768], P('dp')
- grad_tokens: float32 [32768, 768], P('dp')
- grad_w_qkv: float32 [768, 2304], P('dp')
- grad_w_out: float32 [768, 768], P('dp')
- grad_w_up: float32 [768, 3072], P('dp')
- grad_w_down: float32 [3072, 768], P('dp')
- grad_attn_vectors: float32 [768, 5], P('dp')
- grad_ffn_vectors: float32 [768, 3], P('dp')
- grad_up_bias: float32 [3072], P('dp')
Inputs may be any that keep to these rules, and one draw needn't show every extreme that they name: `lengths`: each sequence has 256 to 1024 real tokens; at least one sequence fills all its slots.
All inputs are finite; a program needn't handle non-finite values. No bound on the sum of `drops` on one device may be relied on, other than what follows from the above.
Results may differ from a plain program's by a relative error of at most 0.014.
The roundings to bfloat16 on the way count: a program that leaves them out, or rounds other values in their place, can miss the bound.
Values may be sent and summed in bfloat16 or wider, within the bound.
A program may use at most 256 MiB of HBM per device.

v0:
```python
import jax
import jax.numpy as jnp
from jax import lax
from jax.sharding import PartitionSpec as P

H = 12
BLOCK = 512


EPSILON = 1e-05
NEGATIVE = -1e30


def normalize(hidden, gain_vec, shift_vec):
    row_mean = jnp.mean(hidden, axis=-1, keepdims=True)
    centered = hidden - row_mean
    variance = jnp.mean(centered * centered, axis=-1, keepdims=True)
    return centered * lax.rsqrt(variance + EPSILON) * gain_vec + shift_vec


def gelu_exact(inputs):
    return jax.nn.gelu(inputs, approximate=False)


def local(
    tokens,
    lengths,
    drops,
    cotangent,
    w_qkv,
    w_out,
    w_up,
    w_down,
    attn_vectors,
    ffn_vectors,
    up_bias,
):
    f32 = jnp.float32
    bf16 = jnp.bfloat16
    seq_len, width = tokens.shape
    head_dim = width // H
    inv_root = head_dim ** (-0.5)
    n_blocks = seq_len // BLOCK
    positions = jnp.arange(seq_len, dtype=jnp.int32)
    key_live = positions < lengths[0]
    valid = key_live.astype(f32)[:, None]
    keep_flag = (1 - drops[0]).astype(f32)
    qkv_full, out_full, avec_low = (
        lax.all_gather(w_qkv, "dp", axis=0, tiled=True),
        lax.all_gather(w_out, "dp", axis=0, tiled=True),
        lax.all_gather(attn_vectors, "dp", axis=0, tiled=True),
    )
    up_full, down_full, fvec_low, bias_low = (
        lax.all_gather(w_up, "dp", axis=0, tiled=True),
        lax.all_gather(w_down, "dp", axis=0, tiled=True),
        lax.all_gather(ffn_vectors, "dp", axis=0, tiled=True),
        lax.all_gather(up_bias, "dp", axis=0, tiled=True),
    )
    avec = avec_low.astype(f32)
    fvec = fvec_low.astype(f32)
    bias_up = bias_low.astype(f32)
    inputs = tokens.astype(f32)
    qkv_bias = jnp.concatenate([avec[:, 0], jnp.zeros((width,), f32), avec[:, 1]])
    projected = (jnp.dot(tokens, qkv_full, preferred_element_type=f32) + qkv_bias).astype(bf16)
    queries = projected[:, :width].reshape(n_blocks, BLOCK, H, head_dim)
    keys_all = projected[:, width : 2 * width].reshape(seq_len, H, head_dim)
    values_all = projected[:, 2 * width :].reshape(seq_len, H, head_dim)

    def scores_of(query_block):
        raw_scores = (
            jnp.einsum("bhd,khd->hbk", query_block, keys_all, preferred_element_type=f32) * inv_root
        )
        return jnp.where(key_live[None, None, :], raw_scores, NEGATIVE)

    def attend(query_block):
        scores = scores_of(query_block)
        top_score = jnp.max(scores, axis=-1, keepdims=True)
        expo = jnp.exp(scores - top_score)
        totals = jnp.sum(expo, axis=-1, keepdims=True)
        probs = (expo / totals).astype(bf16)
        mixed = jnp.einsum("hbk,khd->bhd", probs, values_all, preferred_element_type=f32)
        return (mixed, top_score[..., 0] + jnp.log(totals[..., 0]))

    mixed, log_sums = lax.map(attend, queries)
    heads_out = mixed.reshape(seq_len, width).astype(bf16)
    attn_res = jnp.dot(heads_out, out_full, preferred_element_type=f32) + avec[:, 2]
    first_sum = inputs + attn_res
    normed_one, norm_one_back = jax.vjp(normalize, first_sum, avec[:, 3], avec[:, 4])
    normed_low = normed_one.astype(bf16)
    pre_act = jnp.dot(normed_low, up_full, preferred_element_type=f32) + bias_up
    activated, gelu_back = jax.vjp(gelu_exact, pre_act)
    act_low = activated.astype(bf16)
    ffn_res = jnp.dot(act_low, down_full, preferred_element_type=f32) + fvec[:, 0]
    second_sum = normed_one + ffn_res
    layer_out, norm_two_back = jax.vjp(normalize, second_sum, fvec[:, 1], fvec[:, 2])
    result = (valid * (keep_flag * layer_out + (1 - keep_flag) * inputs)).astype(bf16)
    up_full, down_full = (
        lax.all_gather(w_up, "dp", axis=0, tiled=True),
        lax.all_gather(w_down, "dp", axis=0, tiled=True),
    )
    grad_output = valid * cotangent.astype(f32)
    grad_layer = keep_flag * grad_output
    grad_second, grad_gain_two, grad_shift_two = norm_two_back(grad_layer)
    grad_ffn = grad_second.astype(bf16)
    grad_down = jnp.einsum("tf,td->fd", act_low, grad_ffn, preferred_element_type=f32)
    grad_bias_two = jnp.sum(grad_ffn, axis=0, dtype=f32)
    ffn_vec_grad = jnp.stack([grad_bias_two, grad_gain_two, grad_shift_two], axis=1)
    grad_act = jnp.einsum("td,fd->tf", grad_ffn, down_full, preferred_element_type=f32)
    grad_pre = gelu_back(grad_act)[0].astype(bf16)
    grad_up = jnp.einsum("td,tf->df", normed_low, grad_pre, preferred_element_type=f32)
    grad_bias_up = jnp.sum(grad_pre, axis=0, dtype=f32)
    grad_normed = grad_second + jnp.einsum(
        "tf,df->td", grad_pre, up_full, preferred_element_type=f32
    )
    sum_up, sum_down, sum_fvec, sum_bias_up = (
        lax.psum_scatter(grad_up, "dp", scatter_dimension=0, tiled=True),
        lax.psum_scatter(grad_down, "dp", scatter_dimension=0, tiled=True),
        lax.psum_scatter(ffn_vec_grad, "dp", scatter_dimension=0, tiled=True),
        lax.psum_scatter(grad_bias_up, "dp", scatter_dimension=0, tiled=True),
    )
    qkv_full, out_full = (
        lax.all_gather(w_qkv, "dp", axis=0, tiled=True),
        lax.all_gather(w_out, "dp", axis=0, tiled=True),
    )
    grad_first, grad_gain_one, grad_shift_one = norm_one_back(grad_normed)
    grad_attn = grad_first.astype(bf16)
    grad_bias_out = jnp.sum(grad_attn, axis=0, dtype=f32)
    grad_wout = jnp.einsum("td,te->de", heads_out, grad_attn, preferred_element_type=f32)
    grad_heads = jnp.einsum("te,de->td", grad_attn, out_full, preferred_element_type=f32).astype(
        bf16
    )
    grad_heads = grad_heads.reshape(n_blocks, BLOCK, H, head_dim)

    def back_block(running, block_in):
        grad_keys, grad_values = running
        query_block, grad_block, lse_block = block_in
        scores = scores_of(query_block)
        probs = jnp.exp(scores - lse_block[..., None])
        grad_probs = jnp.einsum("bhd,khd->hbk", grad_block, values_all, preferred_element_type=f32)
        row_delta = jnp.sum(probs * grad_probs, axis=-1, keepdims=True)
        grad_scores = (probs * (grad_probs - row_delta)).astype(bf16)
        grad_query = (
            jnp.einsum("hbk,khd->bhd", grad_scores, keys_all, preferred_element_type=f32) * inv_root
        )
        grad_keys = (
            grad_keys
            + jnp.einsum("hbk,bhd->khd", grad_scores, query_block, preferred_element_type=f32)
            * inv_root
        )
        grad_values = grad_values + jnp.einsum(
            "hbk,bhd->khd", probs.astype(bf16), grad_block, preferred_element_type=f32
        )
        return ((grad_keys, grad_values), grad_query)

    zero_heads = jnp.zeros((seq_len, H, head_dim), f32)
    (grad_keys, grad_values), grad_queries = lax.scan(
        back_block, (zero_heads, zero_heads), (queries, grad_heads, log_sums)
    )
    grad_proj = jnp.concatenate(
        [
            grad_queries.reshape(seq_len, width),
            grad_keys.reshape(seq_len, width),
            grad_values.reshape(seq_len, width),
        ],
        axis=1,
    ).astype(bf16)
    grad_qkv = jnp.einsum("td,te->de", tokens, grad_proj, preferred_element_type=f32)
    proj_sums = jnp.sum(grad_proj, axis=0, dtype=f32)
    attn_vec_grad = jnp.stack(
        [proj_sums[:width], proj_sums[2 * width :], grad_bias_out, grad_gain_one, grad_shift_one],
        axis=1,
    )
    sum_qkv, sum_wout, sum_avec = (
        lax.psum_scatter(grad_qkv, "dp", scatter_dimension=0, tiled=True),
        lax.psum_scatter(grad_wout, "dp", scatter_dimension=0, tiled=True),
        lax.psum_scatter(attn_vec_grad, "dp", scatter_dimension=0, tiled=True),
    )
    grad_inputs = grad_first + jnp.einsum(
        "te,de->td", grad_proj, qkv_full, preferred_element_type=f32
    )
    grad_tokens = keep_flag * grad_inputs + (1 - keep_flag) * grad_output
    return (
        result,
        grad_tokens,
        sum_qkv,
        sum_wout,
        sum_up,
        sum_down,
        sum_avec,
        sum_fvec,
        sum_bias_up,
    )


def solution(mesh):
    return jax.shard_map(
        local,
        mesh=mesh,
        in_specs=(
            P("dp", None),
            P("dp"),
            P("dp"),
            P("dp", None),
            P("dp", None),
            P("dp", None),
            P("dp", None),
            P("dp", None),
            P("dp", None),
            P("dp", None),
            P("dp"),
        ),
        out_specs=(
            P("dp", None),
            P("dp", None),
            P("dp", None),
            P("dp", None),
            P("dp", None),
            P("dp", None),
            P("dp", None),
            P("dp", None),
            P("dp"),
        ),
        check_vma=False,
    )
```

profile of v0, /device:TPU:0, one launch (start us, length us, event | category | flops | bytes accessed | tf_op | source)
XLA Modules:
  0.0 940.3 jit_solution(17599577348114433237)
XLA Ops:
  12.8 42.3 %all-reduce = bf16[3072]{0:T(1024)(128)(2,1)S(1)} all-reduce(bf16[3072]{0:T(1024)(128)(2,1)S(1)} %dynamic-update-slice), channel_id=1, replica_groups=mesh['dp'=32] {'dp'}, use_global_device_ids=true, to_apply=%add | all-reduce | flops 3072 | bytes 12288
  55.7 40.3 %all-gather.1 = bf16[32,24,3]{1,2,0:T(4,128)(2,1)S(1)} all-gather(bf16[1,24,3]{1,2,0:T(4,128)(2,1)} %bitcast.146), channel_id=1, replica_groups=mesh['dp'=32] {'dp'}, dimensions={0}, use_global_device_ids=true | all-gather | bytes 4752 | tf_op jit(solution)/shard_map/all_gather | solution.py:56
  97.0 37.1 %all-gather = bf16[32,24,5]{1,2,0:T(8,128)(2,1)S(1)} all-gather(bf16[1,24,5]{1,2,0:T(8,128)(2,1)} %bitcast.145), channel_id=1, replica_groups=mesh['dp'=32] {'dp'}, dimensions={0}, use_global_device_ids=true | all-gather | bytes 7920 | tf_op jit(solution)/shard_map/all_gather | solution.py:51
  135.0 2.6 copy.80
  139.4 6.1 add_convert_fusion.1
  151.9 3.8 reshape.147
  158.9 70.3 %while.28 = (s32[]{:T(128)}, bf16[2,512,12,64]{1,3,2,0:T(8,128)(2,1)}, f32[2,12,512]{2,1,0:T(8,128)S(1)}, bf16[2,512,12,64]{1,3,2,0:T(8,128)(2,1)S(1)}, bf16[102...) while((s32[]{:T(128)}, ...), condition=%wide.region_3.4_spmd.clone, body=%wide.region_0.3_spmd.clone.sunk | while | flops 1686105088 | bytes 100118728 | solution.py:84
  159.6 10.2 %fusion.107 = (f32[12,512]{1,0:T(8,128)S(1)}, f32[12,512,1024]{2,1,0:T(8,128)}) fusion(pred[1024]{0:T(1024)(128)(4,1)S(1)} %iota_compare_fusion.5, bf16[1024,12,64]{0,2,1:T(8,128)(2,1)S(1)} %get-tuple-element.476, bf16[2,512,12,64]{1,3,2,0:T(8,128)(2,1)S(1)} %get-tuple-element.475, s32[]{:T(128)S(6)} %copy.107), kind=kOutput, calls=%fused_computation.5.clone.1 | convolution fusion | flops 824174592 | bytes 27550724 | tf_op jit(solution)/shard_map/while/body/eval_jaxpr/bhd,khd->hbk/dot_general | solution.py:71
  169.8 12.0 %fusion.108 = f32[12,512]{1,0:T(8,128)S(1)} fusion(f32[12,512,1024]{2,1,0:T(8,128)} %get-tuple-element.442, f32[12,512]{1,0:T(8,128)S(1)} %get-tuple-element.443, pred[1024]{0:T(1024)(128)(4,1)S(1)} %iota_compare_fusion.5), kind=kLoop, calls=%fused_computation.6.clone.1 | loop fusion | flops 25159680 | bytes 25216000 | tf_op jit(solution)/shard_map/while/body/eval_jaxpr/reduce_sum | solution.py:79
  181.8 11.3 %bitcast_dynamic-update-slice_fusion.6 = bf16[2,512,12,64]{1,3,2,0:T(8,128)(2,1)S(1)} fusion(bf16[2,512,12,64]{1,3,2,0:T(8,128)(2,1)S(1)} %copy-done.15, s32[]{:T(128)S(6)} %copy.107, bf16[1024,12,64]{0,2,1:T(8,128)(2,1)S(1)} %copy-done.5, f32[12,512,1024]{2,1,0:T(8,128)} %get-tuple-element.442, f32[12,512]{1,0:T(8,128)S(1)} %fusion.108, ...), kind=kOutput, calls=%fused_computation.8.clone.1 | convolution fusion | flops 836763648 | bytes 28378116 | tf_op jit(solution)/shard_map/while/body/eval_jaxpr/hbk,khd->bhd/dot_general | solution.py:81
  194.8 10.3 %fusion.107 = (f32[12,512]{1,0:T(8,128)S(1)}, f32[12,512,1024]{2,1,0:T(8,128)}) fusion(pred[1024]{0:T(1024)(128)(4,1)S(1)} %iota_compare_fusion.5, bf16[1024,12,64]{0,2,1:T(8,128)(2,1)S(1)} %get-tuple-element.476, bf16[2,512,12,64]{1,3,2,0:T(8,128)(2,1)S(1)} %get-tuple-element.475, s32[]{:T(128)S(6)} %copy.107), kind=kOutput, calls=%fused_computation.5.clone.1 | convolution fusion | flops 824174592 | bytes 27550724 | tf_op jit(solution)/shard_map/while/body/eval_jaxpr/bhd,khd->hbk/dot_general | solution.py:71
  205.1 11.4 %fusion.108 = f32[12,512]{1,0:T(8,128)S(1)} fusion(f32[12,512,1024]{2,1,0:T(8,128)} %get-tuple-element.442, f32[12,512]{1,0:T(8,128)S(1)} %get-tuple-element.443, pred[1024]{0:T(1024)(128)(4,1)S(1)} %iota_compare_fusion.5), kind=kLoop, calls=%fused_computation.6.clone.1 | loop fusion | flops 25159680 | bytes 25216000 | tf_op jit(solution)/shard_map/while/body/eval_jaxpr/reduce_sum | solution.py:79
  216.5 11.2 %bitcast_dynamic-update-slice_fusion.6 = bf16[2,512,12,64]{1,3,2,0:T(8,128)(2,1)S(1)} fusion(bf16[2,512,12,64]{1,3,2,0:T(8,128)(2,1)S(1)} %copy-done.15, s32[]{:T(128)S(6)} %copy.107, bf16[1024,12,64]{0,2,1:T(8,128)(2,1)S(1)} %copy-done.5, f32[12,512,1024]{2,1,0:T(8,128)} %get-tuple-element.442, f32[12,512]{1,0:T(8,128)S(1)} %fusion.108, ...), kind=kOutput, calls=%fused_computation.8.clone.1 | convolution fusion | flops 836763648 | bytes 28378116 | tf_op jit(solution)/shard_map/while/body/eval_jaxpr/hbk,khd->bhd/dot_general | solution.py:81
  229.3 4.2 copy.77
  235.1 3.8 fusion.60
  239.7 38.3 %multiply_convert_fusion.1 = (bf16[1024,3072]{1,0:T(8,128)(2,1)}, f32[1024,3072]{1,0:T(8,128)}, f32[1024,3072]{1,0:T(8,128)}) fusion(f32[3072]{0:T(1024)S(1)} %copy-done.45, bf16[768,3072]{1,0:T(8,128)(2,1)} %all-gather.11.cloned.1.call-done, f32[1024,768]{0,1:T(8,128)S(1)} %get-tuple-element.337, f32[768]{0:T(1024)S(1)} %copy-done.47, ...), kind=kOutput, calls=%fused_computation.48 | convolution fusion | flops 5043388416 | bytes 39348224 | tf_op jit(solution)/shard_map/dot_general | solution.py:90
  278.0 9.7 %fusion.61 = (f32[1024]{0:T(1024)S(1)}, f32[1024,768]{0,1:T(8,128)S(1)}) fusion(f32[768]{0:T(1024)S(1)} %copy-done.52, bf16[1024,3072]{1,0:T(8,128)(2,1)} %get-tuple-element.322, bf16[3072,768]{1,0:T(8,128)(2,1)} %all-gather.13.cloned.1.call-done, f32[768]{0:T(1024)S(1)} %copy-done.47, f32[768]{0:T(1024)S(1)} %copy-done.36, f32[1024]{0:T(1024)S(1)} %fusion.49, ...), kind=kOutput, calls=%fused_computation.124 | convolution fusion | flops 4837342208 | bytes 17323008 | tf_op jit(solution)/shard_map/dot_general | solution.py:93
  291.1 4.0 convert_reduce_fusion.2
  295.2 18.0 %convert_reduce_fusion = (f32[3072]{0:T(1024)}, bf16[1024,3072]{1,0:T(8,128)(2,1)}) fusion(f32[1024,3072]{1,0:T(8,128)} %get-tuple-element.323, bf16[1024,768]{0,1:T(8,128)(2,1)S(1)} %get-tuple-element.317, bf16[3072,768]{1,0:T(8,128)(2,1)} %all-gather.13.cloned.1.call-done, f32[1024,3072]{1,0:T(8,128)} %get-tuple-element.338, f32[3072]{0:T(1024)S(1)} %copy-done.45), kind=kOutput, calls=%fused_computation.46 | convolution fusion | flops 4885312512 | bytes 37773312 | tf_op jit(solution)/shard_map/td,fd->tf/dot_general | solution.py:108
  313.2 11.7 %multiply_reduce_fusion.2 = (f32[768]{0:T(1024)}, f32[1024]{0:T(1024)S(1)}, f32[768]{0:T(1024)}, f32[1024,768]{0,1:T(8,128)S(1)}) fusion(f32[1024,768]{0,1:T(8,128)} %copy-done.9, f32[1024]{0:T(1024)S(1)} %fusion.49, f32[1024]{0:T(1024)S(1)} %broadcast_multiply_fusion.1, f32[768]{0:T(1024)S(1)} %copy-done.36, bf16[1024,3072]{1,0:T(8,128)(2,1)} %get-tuple-element.343, ...), kind=kOutput, calls=%fused_computation.75 | convolution fusion | flops 4846777344 | bytes 22065156 | tf_op jit(solution)/shard_map/tf,df->td/dot_general | solution.py:112
  328.4 2.9 fusion.62
  331.3 2.7 convolution_convert_fusion
  337.2 3.0 copy.84
  341.6 165.0 %while.29 = (s32[]{:T(128)}, f32[1024,12,64]{0,2,1:T(8,128)}, f32[1024,12,64]{0,2,1:T(8,128)}, bf16[2,512,12,64]{1,3,2,0:T(8,128)(2,1)}, bf16[2,512,12,64]{1,3,2...) while((s32[]{:T(128)}, f32[1024,12,64]{0,2,1:T(8,128)}, ...), condition=%wide.region_14.15_spmd.clone, body=%wide.region_12.14_spmd.clone.sunk | while | flops 4125223936 | bytes 217239728 | solution.py:156
  342.7 10.3 %fusion.118 = f32[12,512,1024]{2,1,0:T(8,128)} fusion(bf16[1024,12,64]{0,2,1:T(8,128)(2,1)S(1)} %get-tuple-element.509, bf16[2,512,12,64]{1,3,2,0:T(8,128)(2,1)S(1)} %get-tuple-element.508, s32[]{:T(128)S(6)} %copy.117), kind=kOutput, calls=%fused_computation.30.clone.1 | convolution fusion | flops 805306368 | bytes 27525124 | tf_op jit(solution)/shard_map/while/body/eval_jaxpr/bhd,khd->hbk/dot_general | solution.py:71
  353.1 13.2 %bitcast_add_fusion.5 = f32[1024,12,64]{0,2,1:T(8,128)} fusion(f32[1024,12,64]{0,2,1:T(8,128)} %get-tuple-element.494, f32[12,512,1024]{2,1,0:T(8,128)} %fusion.118, f32[12,512]{1,0:T(8,128)S(1)} %dynamic-slice_bitcast_fusion.2, pred[1024]{0:T(1024)(128)(4,1)S(1)} %iota_compare_fusion.6, pred[]{:T(512)S(6)} %compare.3, ...), kind=kOutput, calls=%fused_computation.23.clone.1 | convolution fusion | flops 832045056 | bytes 32277508 | tf_op jit(solution)/shard_map/while/body/eval_jaxpr/hbk,bhd->khd/dot_general | solution.py:150
  366.3 17.6 %multiply_reduce_fusion.8 = (f32[12,512]{1,0:T(8,128)S(1)}, f32[12,512,1024]{2,1,0:T(8,128)}) fusion(f32[12,512,1024]{2,1,0:T(8,128)} %fusion.118, f32[12,512]{1,0:T(8,128)S(1)} %dynamic-slice_bitcast_fusion.2, pred[1024]{0:T(1024)(128)(4,1)S(1)} %iota_compare_fusion.6, bf16[1024,12,64]{0,2,1:T(8,128)(2,1)} %get-tuple-element.512, ...), kind=kOutput, calls=%fused_computation.18.clone.1 | convolution fusion | flops 836757504 | bytes 52741124 | tf_op jit(solution)/shard_map/while/body/eval_jaxpr/bhd,khd->hbk/dot_general | solution.py:139
  383.9 22.2 %multiply_convert_fusion.3 = bf16[12,512,1024]{2,1,0:T(8,128)(2,1)} fusion(f32[12,512,1024]{2,1,0:T(8,128)} %get-tuple-element.454, f32[12,512,1024]{2,1,0:T(8,128)} %fusion.118, f32[12,512]{1,0:T(8,128)S(1)} %get-tuple-element.455, f32[12,512]{1,0:T(8,128)S(1)} %dynamic-slice_bitcast_fusion.2, pred[1024]{0:T(1024)(128)(4,1)S(1)} %iota_compare_fusion.6), kind=kLoop, calls=%fused_computation.17.clone.1 | loop fusion | flops 37748736 | bytes 62964736 | tf_op jit(solution)/shard_map/while/body/eval_jaxpr/convert_element_type | solution.py:141
  406.0 9.4 bitcast_dynamic-update-slice_fusion.8
  415.4 8.6 bitcast_add_fusion.4
  424.7 10.2 %fusion.118 = f32[12,512,1024]{2,1,0:T(8,128)} fusion(bf16[1024,12,64]{0,2,1:T(8,128)(2,1)S(1)} %get-tuple-element.509, bf16[2,512,12,64]{1,3,2,0:T(8,128)(2,1)S(1)} %get-tuple-element.508, s32[]{:T(128)S(6)} %copy.117), kind=kOutput, calls=%fused_computation.30.clone.1 | convolution fusion | flops 805306368 | bytes 27525124 | tf_op jit(solution)/shard_map/while/body/eval_jaxpr/bhd,khd->hbk/dot_general | solution.py:71
  434.9 13.8 %bitcast_add_fusion.5 = f32[1024,12,64]{0,2,1:T(8,128)} fusion(f32[1024,12,64]{0,2,1:T(8,128)} %get-tuple-element.494, f32[12,512,1024]{2,1,0:T(8,128)} %fusion.118, f32[12,512]{1,0:T(8,128)S(1)} %dynamic-slice_bitcast_fusion.2, pred[1024]{0:T(1024)(128)(4,1)S(1)} %iota_compare_fusion.6, pred[]{:T(512)S(6)} %compare.3, ...), kind=kOutput, calls=%fused_computation.23.clone.1 | convolution fusion | flops 832045056 | bytes 32277508 | tf_op jit(solution)/shard_map/while/body/eval_jaxpr/hbk,bhd->khd/dot_general | solution.py:150
  448.7 17.4 %multiply_reduce_fusion.8 = (f32[12,512]{1,0:T(8,128)S(1)}, f32[12,512,1024]{2,1,0:T(8,128)}) fusion(f32[12,512,1024]{2,1,0:T(8,128)} %fusion.118, f32[12,512]{1,0:T(8,128)S(1)} %dynamic-slice_bitcast_fusion.2, pred[1024]{0:T(1024)(128)(4,1)S(1)} %iota_compare_fusion.6, bf16[1024,12,64]{0,2,1:T(8,128)(2,1)} %get-tuple-element.512, ...), kind=kOutput, calls=%fused_computation.18.clone.1 | convolution fusion | flops 836757504 | bytes 52741124 | tf_op jit(solution)/shard_map/while/body/eval_jaxpr/bhd,khd->hbk/dot_general | solution.py:139
  466.1 21.5 %multiply_convert_fusion.3 = bf16[12,512,1024]{2,1,0:T(8,128)(2,1)} fusion(f32[12,512,1024]{2,1,0:T(8,128)} %get-tuple-element.454, f32[12,512,1024]{2,1,0:T(8,128)} %fusion.118, f32[12,512]{1,0:T(8,128)S(1)} %get-tuple-element.455, f32[12,512]{1,0:T(8,128)S(1)} %dynamic-slice_bitcast_fusion.2, pred[1024]{0:T(1024)(128)(4,1)S(1)} %iota_compare_fusion.6), kind=kLoop, calls=%fused_computation.17.clone.1 | loop fusion | flops 37748736 | bytes 62964736 | tf_op jit(solution)/shard_map/while/body/eval_jaxpr/convert_element_type | solution.py:141
  487.6 9.4 bitcast_dynamic-update-slice_fusion.8
  497.0 9.4 %bitcast_add_fusion.4 = f32[1024,12,64]{0,2,1:T(8,128)} fusion(f32[1024,12,64]{0,2,1:T(8,128)} %get-tuple-element.493, bf16[12,512,1024]{2,1,0:T(8,128)(2,1)} %multiply_convert_fusion.3, pred[]{:T(512)S(6)} %compare.3, bf16[2,512,12,64]{1,3,2,0:T(8,128)(2,1)S(1)} %get-tuple-element.508, s32[]{:T(128)S(6)} %copy.117), kind=kOutput, calls=%fused_computation.24.clone.1 | convolution fusion | flops 807665664 | bytes 19660804 | tf_op jit(solution)/shard_map/while/body/eval_jaxpr/hbk,bhd->khd/dot_general | solution.py:147
  506.6 3.2 copy.85
  510.5 3.0 convert.14
  514.7 9.2 convolution_bitcast_fusion
  523.9 8.0 copy.92
  533.8 10.7 %fusion.51 = f32[768,3072]{1,0:T(8,128)} fusion(bf16[1024,3072]{1,0:T(8,128)(2,1)} %get-tuple-element.343, f32[1024,768]{0,1:T(8,128)S(1)} %copy-done.11, f32[768]{0:T(1024)S(1)} %copy-done.48, f32[768]{0:T(1024)S(1)} %copy-done.37, f32[1024]{0:T(1024)S(1)} %copy-done.42, f32[1024]{0:T(1024)S(1)} %copy-done.33), kind=kOutput, calls=%fused_computation.117 | convolution fusion | flops 4835770368 | bytes 18888704 | tf_op jit(solution)/shard_map/td,tf->df/dot_general | solution.py:110
  546.0 10.6 %fusion.63 = f32[3072,768]{1,0:T(8,128)} fusion(bf16[1024,3072]{1,0:T(8,128)(2,1)} %get-tuple-element.322, bf16[1024,768]{0,1:T(8,128)(2,1)S(1)} %copy-done.23), kind=kOutput, calls=%fused_computation.126 | convolution fusion | flops 4831838208 | bytes 17301504 | tf_op jit(solution)/shard_map/tf,td->fd/dot_general | solution.py:105
  559.7 10.3 %multiply_add_fusion = f32[1024,768]{0,1:T(8,128)} fusion(bf16[1024,768]{0,1:T(8,128)(2,1)S(1)} %copy-done.7, f32[1024,768]{0,1:T(8,128)} %copy-done.12, bf16[768,2304]{1,0:T(8,128)(2,1)} %all-gather.7.cloned.1.call-done, f32[1024]{0:T(1024)S(1)} %copy-done.44, f32[]{:T(128)S(6)} %sub.55, f32[]{:T(128)} %bitcast.1, f32[1024]{0:T(1024)S(1)} %copy-done.30, ...), kind=kOutput, calls=%fused_computation.77 | convolution fusion | flops 3643539456 | bytes 16130056 | tf_op jit(solution)/shard_map/te,de->td/dot_general | solution.py:178
  570.0 3.7 copy.88
  575.7 39.6 %all-reduce.4 = (f32[768,5]{0,1:T(8,128)S(1)}, f32[768,3]{0,1:T(4,128)S(1)}, f32[3072]{0:T(1024)S(1)}) all-reduce(f32[768,5]{0,1:T(8,128)S(1)} %stack.35, f32[768,3]{0,1:T(4,128)S(1)} %pad_maximum_fusion.2, f32[3072]{0:T(1024)S(1)} %copy-done.46), channel_id=6, replica_groups=mesh['dp'=32] {'dp'}, use_global_device_ids=true, to_apply=%region_23.24.clone | all-reduce | flops 9216 | bytes 73728
  617.2 32.7 %reduce-scatter.15.cloned.1.call-done = f32[24,2304]{1,0:T(8,128)} async-done(((f32[768,2304]{1,0:T(8,128)}), f32[24,2304]{1,0:T(8,128)}) %reduce-scatter.15.cloned.1.call-update) | async-done | bytes 221200
  650.0 141.6 %reduce-scatter.11.cloned.1.call-done = f32[24,3072]{1,0:T(8,128)} async-done(((f32[768,3072]{1,0:T(8,128)}), f32[24,3072]{1,0:T(8,128)}) %reduce-scatter.11.cloned.1.call-update) | async-done | bytes 294928 | tf_op jit(solution)/shard_map/reduce_scatter | solution.py:116
  791.6 141.6 %reduce-scatter.13.cloned.1.call-done = f32[96,768]{1,0:T(8,128)} async-done(((f32[3072,768]{1,0:T(8,128)}), f32[96,768]{1,0:T(8,128)}) %reduce-scatter.13.cloned.1.call-update) | async-done | bytes 294928 | tf_op jit(solution)/shard_map/reduce_scatter | solution.py:117
  (201 shorter events, 48.6 us)
Async XLA Ops:
  7.2 130.5 %copy-start.24 = (bf16[1024,768]{1,0:T(8,128)(2,1)S(1)}, bf16[1024,768]{1,0:T(8,128)(2,1)}, u32[]{:S(2)}) copy-start(bf16[1024,768]{1,0:T(8,128)(2,1)} %param.15) | copy-start | bytes 4718596
  7.2 132.2 %all-gather.7.cloned.1.call-start = ((), (), s32[]{:S(2)}) async-start(), calls=%async_computation.4 | async-start | bytes 3649536 | tf_op jit(solution)/shard_map/all_gather | solution.py:49
  7.9 227.1 %all-gather.9.cloned.1.call-start = ((), (), s32[]{:S(2)}) async-start(), calls=%async_computation.5 | async-start | bytes 1216512 | tf_op jit(solution)/shard_map/all_gather | solution.py:50
  8.7 230.7 %all-gather.11.cloned.1.call-start = ((), (), s32[]{:S(2)}) async-start(), calls=%async_computation.6 | async-start | bytes 4866048 | tf_op jit(solution)/shard_map/all_gather | solution.py:54
  9.4 268.6 %all-gather.13.cloned.1.call-start = ((), (), s32[]{:S(2)}) async-start(), calls=%async_computation.7 | async-start | bytes 4866048 | tf_op jit(solution)/shard_map/all_gather | solution.py:55
  10.0 607.3 %reduce-scatter.9.cloned.1.call-start = ((), (), s32[]{:S(2)}) async-start(), calls=%async_computation.8 | async-start | bytes 2433024 | tf_op jit(solution)/shard_map/reduce_scatter | solution.py:175
  169.8 12.0 %copy-start.5 = (bf16[1024,12,64]{0,2,1:T(8,128)(2,1)S(1)}, bf16[1024,12,64]{0,2,1:T(8,128)(2,1)}, u32[]{:S(2)}) copy-start(bf16[1024,12,64]{0,2,1:T(8,128)(2,1)} %get-tuple-element.477) | copy-start | bytes 4718596 | tf_op jit(solution)/shard_map/while
  169.8 12.0 %copy-start.15 = (bf16[2,512,12,64]{1,3,2,0:T(8,128)(2,1)S(1)}, bf16[2,512,12,64]{1,3,2,0:T(8,128)(2,1)}, u32[]{:S(2)}) copy-start(bf16[2,512,12,64]{1,3,2,0:T(8,128)(2,1)} %get-tuple-element.465) | copy-start | bytes 4718596 | tf_op jit(solution)/shard_map/while
  205.1 11.4 %copy-start.5 = (bf16[1024,12,64]{0,2,1:T(8,128)(2,1)S(1)}, bf16[1024,12,64]{0,2,1:T(8,128)(2,1)}, u32[]{:S(2)}) copy-start(bf16[1024,12,64]{0,2,1:T(8,128)(2,1)} %get-tuple-element.477) | copy-start | bytes 4718596 | tf_op jit(solution)/shard_map/while
  205.1 11.4 %copy-start.15 = (bf16[2,512,12,64]{1,3,2,0:T(8,128)(2,1)S(1)}, bf16[2,512,12,64]{1,3,2,0:T(8,128)(2,1)}, u32[]{:S(2)}) copy-start(bf16[2,512,12,64]{1,3,2,0:T(8,128)(2,1)} %get-tuple-element.465) | copy-start | bytes 4718596 | tf_op jit(solution)/shard_map/while
  229.2 5.8 copy-start
  229.2 5.8 copy-start.3
  229.2 5.8 copy-start.27
  229.3 5.8 copy-start.49
  238.9 39.1 %copy-start.9 = (f32[1024,768]{0,1:T(8,128)}, f32[1024,768]{0,1:T(8,128)S(1)}, u32[]{:S(2)}) copy-start(f32[1024,768]{0,1:T(8,128)S(1)} %get-tuple-element.337) | copy-start | bytes 9437188
  238.9 86.0 %copy-start.32 = (f32[1024]{0:T(1024)}, f32[1024]{0:T(1024)S(1)}, u32[]{:S(2)}) copy-start(f32[1024]{0:T(1024)S(1)} %broadcast_multiply_fusion.1) | copy-start | bytes 12292
  239.3 85.6 %copy-start.41 = (f32[1024]{0:T(1024)}, f32[1024]{0:T(1024)S(1)}, u32[]{:S(2)}) copy-start(f32[1024]{0:T(1024)S(1)} %fusion.49) | copy-start | bytes 12292
  239.7 38.3 %copy-start.52 = (f32[768]{0:T(1024)S(1)}, f32[768]{0:T(1024)}, u32[]{:S(2)}) copy-start(f32[768]{0:T(1024)} %get-tuple-element.278) | copy-start | bytes 9220
  278.0 9.8 %copy-start.6 = (bf16[1024,768]{0,1:T(8,128)(2,1)S(1)}, bf16[1024,768]{0,1:T(8,128)(2,1)}, u32[]{:S(2)}) copy-start(bf16[1024,768]{0,1:T(8,128)(2,1)} %copy.80) | copy-start | bytes 4718596
  278.0 9.8 %copy-start.29 = (f32[1024]{0:T(1024)S(1)}, f32[1024]{0:T(1024)}, u32[]{:S(2)}) copy-start(f32[1024]{0:T(1024)} %fusion.48) | copy-start | bytes 12292
  278.0 9.8 %copy-start.31 = (f32[768]{0:T(1024)S(1)}, f32[768]{0:T(1024)}, u32[]{:S(2)}) copy-start(f32[768]{0:T(1024)} %get-tuple-element.276) | copy-start | bytes 9220
  288.7 2.4 copy-start.14
  288.7 2.4 copy-start.35
  295.2 18.0 %copy-start.22 = (bf16[1024,768]{0,1:T(8,128)(2,1)}, bf16[1024,768]{0,1:T(8,128)(2,1)S(1)}, u32[]{:S(2)}) copy-start(bf16[1024,768]{0,1:T(8,128)(2,1)S(1)} %get-tuple-element.317) | copy-start | bytes 4718596
  313.2 11.7 %copy-start.10 = (f32[1024,768]{0,1:T(8,128)S(1)}, f32[1024,768]{0,1:T(8,128)}, u32[]{:S(2)}) copy-start(f32[1024,768]{0,1:T(8,128)} %copy-done.9) | copy-start | bytes 9437188
  325.7 2.7 copy-start.26
  325.8 2.7 copy-start.43
  337.2 4.4 copy-start.1
  337.2 4.4 copy-start.4
  337.2 4.4 copy-start.28
  340.2 309.7 %reduce-scatter.15.cloned.1.call-start = ((), (), s32[]{:S(2)}) async-start(), calls=%async_computation.11 | async-start | bytes 7299072
  342.7 10.4 %copy-start.8 = (bf16[2,512,12,64]{1,3,2,0:T(8,128)(2,1)S(1)}, bf16[2,512,12,64]{1,3,2,0:T(8,128)(2,1)}, u32[]{:S(2)}) copy-start(bf16[2,512,12,64]{1,3,2,0:T(8,128)(2,1)} %get-tuple-element.511) | copy-start | bytes 4718596 | tf_op jit(solution)/shard_map/while
  424.7 10.2 %copy-start.8 = (bf16[2,512,12,64]{1,3,2,0:T(8,128)(2,1)S(1)}, bf16[2,512,12,64]{1,3,2,0:T(8,128)(2,1)}, u32[]{:S(2)}) copy-start(bf16[2,512,12,64]{1,3,2,0:T(8,128)(2,1)} %get-tuple-element.511) | copy-start | bytes 4718596 | tf_op jit(solution)/shard_map/while
  506.6 3.6 copy-start.2
  510.2 3.3 copy-start.17
  510.4 3.1 copy-start.19
  510.5 4.2 copy-start.25
  531.9 1.9 copy-start.37
  531.9 1.9 copy-start.42
  531.9 259.6 %reduce-scatter.11.cloned.1.call-start = ((), (), s32[]{:S(2)}) async-start(), calls=%async_computation.9 | async-start | bytes 9732096 | tf_op jit(solution)/shard_map/reduce_scatter | solution.py:116
  544.5 388.7 %reduce-scatter.13.cloned.1.call-start = ((), (), s32[]{:S(2)}) async-start(), calls=%async_computation.10 | async-start | bytes 9732096 | tf_op jit(solution)/shard_map/reduce_scatter | solution.py:117
  556.6 3.0 copy-start.40
  556.6 3.0 copy-start.7
  556.6 3.0 copy-start.30
  556.7 3.0 copy-start.44
  570.0 3.7 copy-start.18
  570.0 3.7 copy-start.20
  573.7 2.0 copy-start.46
  (17 other events, 19.6 us)
Sparse Core Ops, SparseCore 0:
  10.9 62.7 all-gather.6
  76.6 52.7 all-gather.8
  132.3 62.4 all-gather.10
  197.6 61.9 all-gather.12
  340.4 96.9 reduce-scatter.8
  532.0 117.8 reduce-scatter.14
  656.4 135.0 reduce-scatter.10
  798.0 135.1 reduce-scatter.12
where the time goes:
time: 950 us; the launch traced here: 940 us
  waiting for transfers between devices  319 us (34%)
  matrix products  296 us (31%)
  blocking collectives  159 us (17%)
  other arithmetic  85.6 us (9%)
  local copies, waits for them, and re-layouts  62.6 us (7%)
  between operations  16.4 us (2%)
    reduce_scatter x1, waiting for transfers between devices, local(): lax.psum_scatter(grad_down, 'dp', scatter_dimension=0, tiled=True)  142 us
    reduce_scatter x1, waiting for transfers between devices, local(): lax.psum_scatter(grad_up, 'dp', scatter_dimension=0, tiled=True)  142 us
    unnamed x2, blocking collectives  81.9 us
    convert_element_type x2, other arithmetic, back_block(): grad_scores = (probs * (grad_probs - row_delta)).astype(bf16)  43.6 us
    dot_general x4, matrix products, scores_of(): jnp.einsum('bhd,khd->hbk', query_block, keys_all, preferred_element_type=...  40.9 us
    all_gather x1, blocking collectives, local(): lax.all_gather(ffn_vectors, 'dp', axis=0, tiled=True)  40.3 us
    dot_general x1, matrix products, local(): pre_act = jnp.dot(normed_low, up_full, preferred_element_type=f32) + bias_up  38.3 us
    all_gather x1, blocking collectives, local(): lax.all_gather(attn_vectors, 'dp', axis=0, tiled=True)  37.1 us
  transfers between devices with their start and end apart: 8, of which 3 were waited for; matrix products, arithmetic and copies ran while one was open for 40% of the time, Pallas kernels for 0%

commit v1 on v0

--- a/solution.py
+++ b/solution.py
@@ -1,7 +1,254 @@
+import functools
+
 import jax
 import jax.numpy as jnp
 from jax import lax
+from jax.experimental import pallas as pl
+from jax.experimental.pallas import tpu as pltpu
 from jax.sharding import PartitionSpec as P
+
+MESH = pl.DeviceIdType.MESH
+GRID = (4, 2, 2, 2)
+LANES = 128
+ANY = pl.BlockSpec(memory_space=pl.ANY)
+VMEM = pl.BlockSpec(memory_space=pltpu.VMEM)
+
+
+def place():
+    me = lax.axis_index("dp")
+    return me // 8, (me // 4) % 2, (me // 2) % 2, me % 2
+
+
+def device(z, y, x, c):
+    return ((z * 2 + y) * 2 + x) * 2 + c
+
+
+def remote(src, dst, send, recv, to):
+    return pltpu.make_async_remote_copy(
+        src_ref=src, dst_ref=dst, send_sem=send, recv_sem=recv, device_id=(to,), device_id_type=MESH
+    )
+
+
+def meet(z, y, x, c):
+    barrier = pltpu.get_barrier_semaphore()
+    others = [device((z + k) % 4, y, x, c) for k in (1, 2, 3)]
+    others += [device(z, 1 - y, x, c), device(z, y, 1 - x, c), device(z, y, x, 1 - c)]
+    for other in others:
+        pl.semaphore_signal(barrier, inc=1, device_id=(other,), device_id_type=MESH)
+    pl.semaphore_wait(barrier, len(others))
+
+
+def gather_kernel(count, *refs):
+    shards, outs = refs[:count], refs[count : 2 * count]
+    send, recv, local = refs[2 * count :]
+    z, y, x, c = place()
+    meet(z, y, x, c)
+    y_to, x_to, c_to = device(z, 1 - y, x, c), device(z, y, 1 - x, c), device(z, y, x, 1 - c)
+    low, high = pl.ds(0, 2), pl.ds(2, 2)
+    every, both = pl.ds(0, 4), pl.ds(0, 2)
+    arrays = range(count)
+
+    def copy(w, slot, where, to):
+        return remote(outs[w].at[where], outs[w].at[where], send.at[w, slot], recv.at[w, slot], to)
+
+    pending = []
+
+    def go(w, slot, where, to):
+        one = copy(w, slot, where, to)
+        one.start()
+        pending.append(one)
+
+    def arrived(w, slot, where):
+        copy(w, slot, where, c_to).wait_recv()
+
+    own = [pltpu.make_async_copy(shards[w], outs[w].at[z, y, x, c], local.at[w]) for w in arrays]
+    for w in arrays:
+        own[w].start()
+        for k in (1, 2, 3):
+            one = remote(
+                shards[w],
+                outs[w].at[z, y, x, c],
+                send.at[w, k - 1],
+                recv.at[w, k - 1],
+                device((z + k) % 4, y, x, c),
+            )
+            one.start()
+            pending.append(one)
+    for w in arrays:
+        own[w].wait()
+        for k in (1, 2, 3):
+            arrived(w, k - 1, ((z + 4 - k) % 4, y, x, c))
+        go(w, 3, (low, y, x, c), x_to)
+        go(w, 4, (high, y, x, c), y_to)
+        go(w, 7, (every, y, x, c), c_to)
+    for w in arrays:
+        arrived(w, 3, (low, y, 1 - x, c))
+        go(w, 5, (low, y, both, c), y_to)
+        go(w, 8, (low, y, 1 - x, c), c_to)
+        arrived(w, 4, (high, 1 - y, x, c))
+        go(w, 6, (high, both, x, c), x_to)
+        go(w, 9, (high, 1 - y, x, c), c_to)
+    for w in arrays:
+        arrived(w, 5, (low, 1 - y, both, c))
+        go(w, 10, (low, 1 - y, both, c), c_to)
+        arrived(w, 6, (high, both, 1 - x, c))
+        go(w, 11, (high, both, 1 - x, c), c_to)
+    for w in arrays:
+        arrived(w, 7, (every, y, x, 1 - c))
+        arrived(w, 8, (low, y, 1 - x, 1 - c))
+        arrived(w, 9, (high, 1 - y, x, 1 - c))
+        arrived(w, 10, (low, 1 - y, both, 1 - c))
+        arrived(w, 11, (high, both, 1 - x, 1 - c))
+    for one in pending:
+        one.wait_send()
+
+
+def gather(shards):
+    count = len(shards)
+    return pl.pallas_call(
+        functools.partial(gather_kernel, count),
+        out_shape=[jax.ShapeDtypeStruct(GRID + s.shape, s.dtype) for s in shards],
+        in_specs=[VMEM] * count,
+        out_specs=[ANY] * count,
+        scratch_shapes=[
+            pltpu.SemaphoreType.DMA((count, 12)),
+            pltpu.SemaphoreType.DMA((count, 12)),
+            pltpu.SemaphoreType.DMA((count,)),
+        ],
+        compiler_params=pltpu.CompilerParams(
+            collective_id=0, has_side_effects=True, vmem_limit_bytes=8 << 20
+        ),
+        name="gather_weights",
+    )(*shards)
+
+
+def scatter_kernel(count, *refs):
+    grads, sums = refs[:count], refs[count : 2 * count]
+    groups = [refs[2 * count + 7 * w : 2 * count + 7 * (w + 1)] for w in range(count)]
+    send, recv, local = refs[9 * count :]
+    z, y, x, c = place()
+    meet(z, y, x, c)
+    y_to, x_to, c_to = device(z, 1 - y, x, c), device(z, y, 1 - x, c), device(z, y, x, 1 - c)
+    low, high = pl.ds(0, 2), pl.ds(2, 2)
+    every, both = pl.ds(0, 4), pl.ds(0, 2)
+    arrays = range(count)
+    f32 = jnp.float32
+    pending = []
+
+    def go(src, dst, w, slot, to):
+        one = remote(src, dst, send.at[w, slot], recv.at[w, slot], to)
+        one.start()
+        pending.append(one)
+        return one
+
+    def add(dst, src, total):
+        def step(i, carry):
+            a, b = dst(i), src(i)
+            a[...] = (a[...].astype(f32) + b[...].astype(f32)).astype(a.dtype)
+            return carry
+
+        lax.fori_loop(0, total, step, 0)
+
+    own, first = [], []
+    for w in arrays:
+        acc, r0 = groups[w][:2]
+        first.append(go(grads[w].at[every, both, both, 1 - c], r0, w, 0, c_to))
+        one = pltpu.make_async_copy(grads[w].at[every, both, both, c], acc, local.at[w])
+        one.start()
+        own.append(one)
+    second = []
+    for w in arrays:
+        acc, r0, r1a, r1b, r2a, r2b, r3 = groups[w]
+        own[w].wait()
+        first[w].wait_recv()
+        add(
+            lambda i: acc.at[i // 4, (i // 2) % 2, i % 2],
+            lambda i: r0.at[i // 4, (i // 2) % 2, i % 2],
+            16,
+        )
+        second.append(
+            (
+                go(acc.at[low, both, 1 - x], r1a, w, 1, x_to),
+                go(acc.at[high, 1 - y, both], r1b, w, 2, y_to),
+            )
+        )
+    third = []
+    for w in arrays:
+        acc, r0, r1a, r1b, r2a, r2b, r3 = groups[w]
+        second[w][0].wait_recv()
+        add(lambda i: acc.at[i // 2, i % 2, x], lambda i: r1a.at[i // 2, i % 2], 4)
+        a = go(acc.at[low, 1 - y, x], r2a, w, 3, y_to)
+        second[w][1].wait_recv()
+        add(lambda i: acc.at[2 + i // 2, y, i % 2], lambda i: r1b.at[i // 2, i % 2], 4)
+        b = go(acc.at[high, y, 1 - x], r2b, w, 4, x_to)
+        third.append((a, b))
+    last = []
+    for w in arrays:
+        acc, r0, r1a, r1b, r2a, r2b, r3 = groups[w]
+        third[w][0].wait_recv()
+        add(lambda i: acc.at[i, y, x], lambda i: r2a.at[i], 2)
+        third[w][1].wait_recv()
+        add(lambda i: acc.at[2 + i, y, x], lambda i: r2b.at[i], 2)
+        last.append(
+            [
+                go(
+                    acc.at[(z + k) % 4, y, x],
+                    r3.at[k - 1],
+                    w,
+                    4 + k,
+                    device((z + k) % 4, y, x, c),
+                )
+                for k in (1, 2, 3)
+            ]
+        )
+    for w in arrays:
+        acc, r0, r1a, r1b, r2a, r2b, r3 = groups[w]
+        for one in last[w]:
+            one.wait_recv()
+        sums[w][...] = (
+            (acc[z, y, x].astype(f32) + r3[0].astype(f32))
+            + (r3[1].astype(f32) + r3[2].astype(f32))
+        )
+    for one in pending:
+        one.wait_send()
+
+
+def scatter(grads):
+    count = len(grads)
+    scratch = []
+    for g in grads:
+        rows = g.shape[4]
+        bf16 = g.dtype
+        for shape in ((4, 2, 2), (4, 2, 2), (2, 2), (2, 2), (2,), (2,), (3,)):
+            scratch.append(pltpu.VMEM(shape + (rows, LANES), bf16))
+    return pl.pallas_call(
+        functools.partial(scatter_kernel, count),
+        out_shape=[jax.ShapeDtypeStruct(g.shape[4:], jnp.float32) for g in grads],
+        in_specs=[ANY] * count,
+        out_specs=[VMEM] * count,
+        scratch_shapes=scratch
+        + [
+            pltpu.SemaphoreType.DMA((count, 8)),
+            pltpu.SemaphoreType.DMA((count, 8)),
+            pltpu.SemaphoreType.DMA((count,)),
+        ],
+        compiler_params=pltpu.CompilerParams(
+            collective_id=1, has_side_effects=True, vmem_limit_bytes=40 << 20
+        ),
+        name="scatter_grads",
+    )(*grads)
+
+
+def as_slabs(grad):
+    rows, cols = grad.shape[0] // 32, grad.shape[1]
+    tiles = grad.reshape(32, rows // 8, 8, cols // LANES, LANES).transpose(0, 1, 3, 2, 4)
+    return tiles.reshape(GRID + (rows * cols // LANES, LANES))
+
+
+def from_slab(slab, rows, cols):
+    tiles = slab.reshape(rows // 8, cols // LANES, 8, LANES).transpose(0, 2, 1, 3)
+    return tiles.reshape(rows, cols)
+
 
 H = 12
 BLOCK = 512
@@ -22,7 +269,50 @@
     return jax.nn.gelu(inputs, approximate=False)
 
 
+def fetch_plain(*shards):
+    return tuple(lax.all_gather(s, "dp", axis=0, tiled=True) for s in shards)
+
+
+def spread_plain(*grads):
+    return tuple(lax.psum_scatter(g, "dp", scatter_dimension=0, tiled=True) for g in grads)
+
+
+def fetch_kernel(w_qkv, w_out, w_up, w_down, attn_vectors, ffn_vectors, up_bias):
+    small = jnp.concatenate([attn_vectors.reshape(-1), ffn_vectors.reshape(-1), up_bias])
+    small = jnp.pad(small, (0, 16 * LANES - small.shape[0])).reshape(16, LANES)
+    full = gather([w_qkv, w_out, w_up, w_down, small])
+    weights = [f.reshape(-1, f.shape[-1]) for f in full[:4]]
+    small = full[4].reshape(32, 16 * LANES)
+    return (
+        *weights,
+        small[:, :120].reshape(-1, 5),
+        small[:, 120:192].reshape(-1, 3),
+        small[:, 192:288].reshape(-1),
+    )
+
+
+def spread_kernel(g_qkv, g_out, g_up, g_down, g_avec, g_fvec, g_bias):
+    small = jnp.concatenate(
+        [g_avec.reshape(32, 120), g_fvec.reshape(32, 72), g_bias.reshape(32, 96)], axis=1
+    )
+    small = jnp.pad(small, ((0, 0), (0, 16 * LANES - 288))).astype(jnp.bfloat16)
+    big = [as_slabs(g.astype(jnp.bfloat16)) for g in (g_qkv, g_out, g_up, g_down)]
+    s_qkv, s_out, s_up, s_down, s_small = scatter(big + [small.reshape(GRID + (16, LANES))])
+    flat = s_small.reshape(-1)
+    return (
+        from_slab(s_qkv, 24, 2304),
+        from_slab(s_out, 24, 768),
+        from_slab(s_up, 24, 3072),
+        from_slab(s_down, 96, 768),
+        flat[:120].reshape(24, 5),
+        flat[120:192].reshape(24, 3),
+        flat[192:288],
+    )
+
+
 def local(
+    fetch,
+    spread,
     tokens,
     lengths,
     drops,
@@ -45,16 +335,8 @@
     key_live = positions < lengths[0]
     valid = key_live.astype(f32)[:, None]
     keep_flag = (1 - drops[0]).astype(f32)
-    qkv_full, out_full, avec_low = (
-        lax.all_gather(w_qkv, "dp", axis=0, tiled=True),
-        lax.all_gather(w_out, "dp", axis=0, tiled=True),
-        lax.all_gather(attn_vectors, "dp", axis=0, tiled=True),
-    )
-    up_full, down_full, fvec_low, bias_low = (
-        lax.all_gather(w_up, "dp", axis=0, tiled=True),
-        lax.all_gather(w_down, "dp", axis=0, tiled=True),
-        lax.all_gather(ffn_vectors, "dp", axis=0, tiled=True),
-        lax.all_gather(up_bias, "dp", axis=0, tiled=True),
+    (qkv_full, out_full, up_full, down_full, avec_low, fvec_low, bias_low) = fetch(
+        w_qkv, w_out, w_up, w_down, attn_vectors, ffn_vectors, up_bias
     )
     avec = avec_low.astype(f32)
     fvec = fvec_low.astype(f32)
@@ -94,10 +376,6 @@
     second_sum = normed_one + ffn_res
     layer_out, norm_two_back = jax.vjp(normalize, second_sum, fvec[:, 1], fvec[:, 2])
     result = (valid * (keep_flag * layer_out + (1 - keep_flag) * inputs)).astype(bf16)
-    up_full, down_full = (
-        lax.all_gather(w_up, "dp", axis=0, tiled=True),
-        lax.all_gather(w_down, "dp", axis=0, tiled=True),
-    )
     grad_output = valid * cotangent.astype(f32)
     grad_layer = keep_flag * grad_output
     grad_second, grad_gain_two, grad_shift_two = norm_two_back(grad_layer)
@@ -112,16 +390,6 @@
     grad_normed = grad_second + jnp.einsum(
         "tf,df->td", grad_pre, up_full, preferred_element_type=f32
     )
-    sum_up, sum_down, sum_fvec, sum_bias_up = (
-        lax.psum_scatter(grad_up, "dp", scatter_dimension=0, tiled=True),
-        lax.psum_scatter(grad_down, "dp", scatter_dimension=0, tiled=True),
-        lax.psum_scatter(ffn_vec_grad, "dp", scatter_dimension=0, tiled=True),
-        lax.psum_scatter(grad_bias_up, "dp", scatter_dimension=0, tiled=True),
-    )
-    qkv_full, out_full = (
-        lax.all_gather(w_qkv, "dp", axis=0, tiled=True),
-        lax.all_gather(w_out, "dp", axis=0, tiled=True),
-    )
     grad_first, grad_gain_one, grad_shift_one = norm_one_back(grad_normed)
     grad_attn = grad_first.astype(bf16)
     grad_bias_out = jnp.sum(grad_attn, axis=0, dtype=f32)
@@ -170,10 +438,8 @@
         [proj_sums[:width], proj_sums[2 * width :], grad_bias_out, grad_gain_one, grad_shift_one],
         axis=1,
     )
-    sum_qkv, sum_wout, sum_avec = (
-        lax.psum_scatter(grad_qkv, "dp", scatter_dimension=0, tiled=True),
-        lax.psum_scatter(grad_wout, "dp", scatter_dimension=0, tiled=True),
-        lax.psum_scatter(attn_vec_grad, "dp", scatter_dimension=0, tiled=True),
+    sum_qkv, sum_wout, sum_up, sum_down, sum_avec, sum_fvec, sum_bias_up = spread(
+        grad_qkv, grad_wout, grad_up, grad_down, attn_vec_grad, ffn_vec_grad, grad_bias_up
     )
     grad_inputs = grad_first + jnp.einsum(
         "te,de->td", grad_proj, qkv_full, preferred_element_type=f32
@@ -193,8 +459,12 @@
 
 
 def solution(mesh):
+    kernels = mesh.shape["dp"] == 32
+    layer = functools.partial(
+        local, fetch_kernel if kernels else fetch_plain, spread_kernel if kernels else spread_plain
+    )
     return jax.shard_map(
-        local,
+        layer,
         mesh=mesh,
         in_specs=(
             P("dp", None),

time: 950 us -> 647 us (0.68)
  waiting for transfers between devices: 319 us -> 0 us
  Pallas kernels: 0 us -> 186 us
  blocking collectives: 159 us -> 0 us
  local copies, waits for them, and re-layouts: 62.6 us -> 84.1 us
  matrix products: 296 us -> 275 us
  between operations: 16.4 us -> 3.23 us
    reduce_scatter x3 -> x0, waiting for transfers between devices: 283 us -> none  [the longest x1 142 us: local(): lax.psum_scatter(grad_down, 'dp', scatter_dimension=0, tiled=True)]
    pallas_call x0 -> x2, Pallas kernels: none -> 186 us  [the longest x1 95.4 us: scatter(): pl.pallas_call(functools.partial(scatter_kernel, count), out_shape=[jax.S...]
    unnamed x2 -> x0, blocking collectives: 81.9 us -> none
    all_gather x2 -> x0, blocking collectives: 77.4 us -> none  [the longest x1 40.3 us: local(): lax.all_gather(ffn_vectors, 'dp', axis=0, tiled=True)]
    unnamed x9 -> x0, waiting for transfers between devices: 35.4 us -> none
    unnamed x112 -> x140, local copies, waits for them, and re-layouts: 35 us -> 45.1 us
  transfers between devices with their start and end apart: 8 -> 0, of which waited for: 3 -> 0; matrix products, arithmetic and copies ran while one was open for 40% -> 0% of each run, Pallas kernels for 0% -> 0%
where the time goes in v1:
time: 647 us; the launch traced here: 638 us
  matrix products  275 us (43%)
  Pallas kernels  186 us (29%)
  other arithmetic  88.5 us (14%)
  local copies, waits for them, and re-layouts  84.1 us (13%)
    pallas_call x1, Pallas kernels, scatter(): pl.pallas_call(functools.partial(scatter_kernel, count), out_shape=[jax.S...  95.4 us
    pallas_call x1, Pallas kernels, gather(): pl.pallas_call(functools.partial(gather_kernel, count), out_shape=[jax.Sh...  90.9 us
    unnamed x140, local copies, waits for them, and re-layouts  45.1 us
    convert_element_type x2, other arithmetic, back_block(): grad_scores = (probs * (grad_probs - row_delta)).astype(bf16)  42.9 us
    dot_general x4, matrix products, scores_of(): jnp.einsum('bhd,khd->hbk', query_block, keys_all, preferred_element_type=...  40.4 us
    dot_general x1, matrix products, local(): pre_act = jnp.dot(normed_low, up_full, preferred_element_type=f32) + bias_up  39.7 us
    dot_general x2, matrix products, back_block(): jnp.einsum('bhd,khd->hbk', grad_block, values_all, preferred_element_type...  34.8 us
    dot_general x2, matrix products, back_block(): jnp.einsum('hbk,bhd->khd', probs.astype(bf16), grad_block, preferred_elem...  26.9 us

profile of v1, /device:TPU:0, one launch (start us, length us, event | category | flops | bytes accessed | tf_op | source)
XLA Modules:
  0.0 637.8 jit_solution(10328727991596801286)
XLA Ops:
  5.2 2.7 copy.39
  9.5 90.9 %gather_weights.1 = (bf16[4,2,2,2,24,2304]{5,4,3,2,1,0:T(8,128)(2,1)S(1)}, bf16[4,2,2,2,24,768]{5,4,3,2,1,0:T(8,128)(2,1)S(1)}, bf16[4,2,2,2,24,3072]{5,4,3,2,1,...) custom-call(bf16[24,2304]{1,0:T(8,128)(2,1)S(1)} %copy-done.7, ...), custom_call_target="tpu_custom_call" | custom-call | tf_op jit(solution)/shard_map/gather_weights/pallas_call | solution.py:108
  100.4 2.2 copy-done.10
  102.6 2.2 copy-done.11
  112.9 4.2 slice_reduce_fusion.1
  117.2 6.2 fusion.41
  125.1 2.3 reshape.262
  130.5 69.3 %while.28 = (s32[]{:T(128)}, bf16[2,512,12,64]{1,3,2,0:T(8,128)(2,1)}, f32[2,12,512]{2,1,0:T(8,128)}, bf16[2,512,12,64]{1,3,2,0:T(8,128)(2,1)S(1)}, bf16[1024,12...) while((s32[]{:T(128)}, ...), condition=%wide.region_3.4_spmd.clone, body=%wide.region_0.3_spmd.clone.sunk | while | flops 1686105088 | bytes 100102344 | solution.py:366
  131.1 10.1 %fusion.122 = (f32[12,512]{1,0:T(8,128)S(1)}, f32[12,512,1024]{2,1,0:T(8,128)}) fusion(pred[1024]{0:T(1024)(128)(4,1)S(1)} %iota_compare_fusion.7, bf16[1024,12,64]{0,2,1:T(8,128)(2,1)S(1)} %get-tuple-element.446, bf16[2,512,12,64]{1,3,2,0:T(8,128)(2,1)S(1)} %get-tuple-element.445, s32[]{:T(128)S(6)} %copy.67), kind=kOutput, calls=%fused_computation.5.clone.1 | convolution fusion | flops 824174592 | bytes 27550724 | tf_op jit(solution)/shard_map/while/body/eval_jaxpr/bhd,khd->hbk/dot_general | solution.py:353
  141.3 11.4 %fusion.123 = f32[12,512]{1,0:T(8,128)S(1)} fusion(f32[12,512,1024]{2,1,0:T(8,128)} %get-tuple-element.412, f32[12,512]{1,0:T(8,128)S(1)} %get-tuple-element.413, pred[1024]{0:T(1024)(128)(4,1)S(1)} %iota_compare_fusion.7), kind=kLoop, calls=%fused_computation.6.clone.1 | loop fusion | flops 25159680 | bytes 25216000 | tf_op jit(solution)/shard_map/while/body/eval_jaxpr/reduce_sum | solution.py:361
  152.7 11.2 %bitcast_dynamic-update-slice_fusion.6 = bf16[2,512,12,64]{1,3,2,0:T(8,128)(2,1)S(1)} fusion(bf16[2,512,12,64]{1,3,2,0:T(8,128)(2,1)S(1)} %copy-done.35, s32[]{:T(128)S(6)} %copy.67, bf16[1024,12,64]{0,2,1:T(8,128)(2,1)S(1)} %copy-done.23, f32[12,512,1024]{2,1,0:T(8,128)} %get-tuple-element.412, f32[12,512]{1,0:T(8,128)S(1)} %fusion.123, ...), kind=kOutput, calls=%fused_computation.8.clone.1 | convolution fusion | flops 836763648 | bytes 28378116 | tf_op jit(solution)/shard_map/while/body/eval_jaxpr/hbk,khd->bhd/dot_general | solution.py:363
  165.7 10.1 %fusion.122 = (f32[12,512]{1,0:T(8,128)S(1)}, f32[12,512,1024]{2,1,0:T(8,128)}) fusion(pred[1024]{0:T(1024)(128)(4,1)S(1)} %iota_compare_fusion.7, bf16[1024,12,64]{0,2,1:T(8,128)(2,1)S(1)} %get-tuple-element.446, bf16[2,512,12,64]{1,3,2,0:T(8,128)(2,1)S(1)} %get-tuple-element.445, s32[]{:T(128)S(6)} %copy.67), kind=kOutput, calls=%fused_computation.5.clone.1 | convolution fusion | flops 824174592 | bytes 27550724 | tf_op jit(solution)/shard_map/while/body/eval_jaxpr/bhd,khd->hbk/dot_general | solution.py:353
  175.8 11.4 %fusion.123 = f32[12,512]{1,0:T(8,128)S(1)} fusion(f32[12,512,1024]{2,1,0:T(8,128)} %get-tuple-element.412, f32[12,512]{1,0:T(8,128)S(1)} %get-tuple-element.413, pred[1024]{0:T(1024)(128)(4,1)S(1)} %iota_compare_fusion.7), kind=kLoop, calls=%fused_computation.6.clone.1 | loop fusion | flops 25159680 | bytes 25216000 | tf_op jit(solution)/shard_map/while/body/eval_jaxpr/reduce_sum | solution.py:361
  187.2 11.2 %bitcast_dynamic-update-slice_fusion.6 = bf16[2,512,12,64]{1,3,2,0:T(8,128)(2,1)S(1)} fusion(bf16[2,512,12,64]{1,3,2,0:T(8,128)(2,1)S(1)} %copy-done.35, s32[]{:T(128)S(6)} %copy.67, bf16[1024,12,64]{0,2,1:T(8,128)(2,1)S(1)} %copy-done.23, f32[12,512,1024]{2,1,0:T(8,128)} %get-tuple-element.412, f32[12,512]{1,0:T(8,128)S(1)} %fusion.123, ...), kind=kOutput, calls=%fused_computation.8.clone.1 | convolution fusion | flops 836763648 | bytes 28378116 | tf_op jit(solution)/shard_map/while/body/eval_jaxpr/hbk,khd->bhd/dot_general | solution.py:363
  199.8 4.2 copy.38
  208.9 39.7 %multiply_convert_fusion.1 = (bf16[1024,3072]{1,0:T(8,128)(2,1)S(1)}, f32[1024,3072]{1,0:T(8,128)}, f32[1024,3072]{1,0:T(8,128)}) fusion(f32[3072]{0:T(1024)S(1)} %copy-done.52, bf16[768,3072]{1,0:T(8,128)(2,1)S(1)} %bitcast.188, f32[1024,768]{0,1:T(8,128)S(1)} %get-tuple-element.302, f32[768]{0:T(1024)S(1)} %copy-done.54, f32[768]{0:T(1024)S(1)} %copy-done.48, ...), kind=kOutput, calls=%fused_computation.47 | convolution fusion | flops 5043388416 | bytes 39348224 | tf_op jit(solution)/shard_map/dot_general | solution.py:372
  248.6 5.9 fusion.77
  255.6 3.7 multiply_reduce_fusion.1
  259.3 2.6 copy.49
  261.9 4.5 fusion.71
  266.4 18.6 %fusion.78 = (bf16[3072]{0:T(1024)(128)(2,1)S(1)}, bf16[1024,3072]{1,0:T(8,128)(2,1)}) fusion(f32[1024,3072]{1,0:T(8,128)} %get-tuple-element.288, bf16[1024,768]{0,1:T(8,128)(2,1)} %get-tuple-element.284, bf16[3072,768]{1,0:T(8,128)(2,1)} %bitcast.192, f32[1024,3072]{1,0:T(8,128)} %get-tuple-element.303, f32[3072]{0:T(1024)S(1)} %copy-done.52), kind=kOutput, calls=%fused_computation.144 | convolution fusion | flops 4882166784 | bytes 37767168 | tf_op jit(solution)/shard_map/td,fd->tf/dot_general | solution.py:386
  285.0 9.7 %convolution_convert_fusion = bf16[3072,768]{1,0:T(8,128)(2,1)} fusion(bf16[1024,3072]{1,0:T(8,128)(2,1)} %copy-done.58, bf16[1024,768]{0,1:T(8,128)(2,1)} %get-tuple-element.284), kind=kOutput, calls=%fused_computation.62 | convolution fusion | flops 4834197504 | bytes 12582912 | tf_op jit(solution)/shard_map/tf,td->fd/dot_general | solution.py:383
  294.7 7.0 %multiply_reduce_fusion.2 = (bf16[768]{0:T(1024)(128)(2,1)S(1)}, f32[1024]{0:T(1024)S(1)}, bf16[768]{0:T(1024)(128)(2,1)S(1)}, f32[1024,768]{0,1:T(8,128)S(1)}) fusion(f32[1024,768]{0,1:T(8,128)S(1)} %copy-done.32, f32[1024]{0:T(1024)S(1)} %fusion.63, f32[1024]{0:T(1024)S(1)} %broadcast_multiply_fusion.1, f32[768]{0:T(1024)S(1)} %copy-done.48, ...), kind=kOutput, calls=%fused_computation.76 | convolution fusion | flops 4846777344 | bytes 22062084 | tf_op jit(solution)/shard_map/tf,df->td/dot_general | solution.py:390
  302.5 7.2 %convolution_convert_fusion.1 = bf16[768,3072]{1,0:T(8,128)(2,1)} fusion(bf16[1024,3072]{1,0:T(8,128)(2,1)S(1)} %copy-done.57, f32[1024,768]{0,1:T(8,128)S(1)} %copy-done.32, f32[768]{0:T(1024)S(1)} %copy-done.54, f32[768]{0:T(1024)S(1)} %copy-done.48, f32[1024]{0:T(1024)S(1)} %fusion.63, f32[1024]{0:T(1024)S(1)} %broadcast_multiply_fusion.1), kind=kOutput, calls=%fused_computation.63 | convolution fusion | flops 4838129664 | bytes 14170112 | tf_op jit(solution)/shard_map/td,tf->df/dot_general | solution.py:388
  314.0 2.5 convolution_convert_fusion.4
  319.3 2.4 reshape.268
  321.7 3.1 copy.43
  326.1 163.2 %while.29 = (s32[]{:T(128)}, f32[1024,12,64]{0,2,1:T(8,128)}, f32[1024,12,64]{0,2,1:T(8,128)}, bf16[2,512,12,64]{1,3,2,0:T(8,128)(2,1)}, bf16[2,512,12,64]{1,3,2...) while((s32[]{:T(128)}, f32[1024,12,64]{0,2,1:T(8,128)}, ...), condition=%wide.region_14.15_spmd.clone, body=%wide.region_12.14_spmd.clone.sunk | while | flops 4125223936 | bytes 217239728 | solution.py:424
  327.0 10.1 %fusion.133 = f32[12,512,1024]{2,1,0:T(8,128)} fusion(bf16[1024,12,64]{0,2,1:T(8,128)(2,1)S(1)} %get-tuple-element.479, bf16[2,512,12,64]{1,3,2,0:T(8,128)(2,1)S(1)} %get-tuple-element.478, s32[]{:T(128)S(6)} %copy.77), kind=kOutput, calls=%fused_computation.30.clone.1 | convolution fusion | flops 805306368 | bytes 27525124 | tf_op jit(solution)/shard_map/while/body/eval_jaxpr/bhd,khd->hbk/dot_general | solution.py:353
  337.1 13.0 %bitcast_add_fusion.5 = f32[1024,12,64]{0,2,1:T(8,128)} fusion(f32[1024,12,64]{0,2,1:T(8,128)} %get-tuple-element.464, f32[12,512,1024]{2,1,0:T(8,128)} %fusion.133, f32[12,512]{1,0:T(8,128)S(1)} %dynamic-slice_bitcast_fusion.2, pred[1024]{0:T(1024)(128)(4,1)S(1)} %iota_compare_fusion.8, pred[]{:T(512)S(6)} %compare.45, ...), kind=kOutput, calls=%fused_computation.23.clone.1 | convolution fusion | flops 832045056 | bytes 32277508 | tf_op jit(solution)/shard_map/while/body/eval_jaxpr/hbk,bhd->khd/dot_general | solution.py:418
  350.1 17.4 %multiply_reduce_fusion.8 = (f32[12,512]{1,0:T(8,128)S(1)}, f32[12,512,1024]{2,1,0:T(8,128)}) fusion(f32[12,512,1024]{2,1,0:T(8,128)} %fusion.133, f32[12,512]{1,0:T(8,128)S(1)} %dynamic-slice_bitcast_fusion.2, pred[1024]{0:T(1024)(128)(4,1)S(1)} %iota_compare_fusion.8, bf16[1024,12,64]{0,2,1:T(8,128)(2,1)} %get-tuple-element.482, ...), kind=kOutput, calls=%fused_computation.18.clone.1 | convolution fusion | flops 836757504 | bytes 52741124 | tf_op jit(solution)/shard_map/while/body/eval_jaxpr/bhd,khd->hbk/dot_general | solution.py:407
  367.5 21.4 %multiply_convert_fusion.3 = bf16[12,512,1024]{2,1,0:T(8,128)(2,1)} fusion(f32[12,512,1024]{2,1,0:T(8,128)} %get-tuple-element.424, f32[12,512,1024]{2,1,0:T(8,128)} %fusion.133, f32[12,512]{1,0:T(8,128)S(1)} %get-tuple-element.425, f32[12,512]{1,0:T(8,128)S(1)} %dynamic-slice_bitcast_fusion.2, pred[1024]{0:T(1024)(128)(4,1)S(1)} %iota_compare_fusion.8), kind=kLoop, calls=%fused_computation.17.clone.1 | loop fusion | flops 37748736 | bytes 62964736 | tf_op jit(solution)/shard_map/while/body/eval_jaxpr/convert_element_type | solution.py:409
  388.9 9.4 %bitcast_dynamic-update-slice_fusion.8 = bf16[2,512,12,64]{1,3,2,0:T(8,128)(2,1)} fusion(bf16[2,512,12,64]{1,3,2,0:T(8,128)(2,1)} %get-tuple-element.465, s32[]{:T(128)S(6)} %copy.77, bf16[12,512,1024]{2,1,0:T(8,128)(2,1)} %multiply_convert_fusion.3, bf16[1024,12,64]{0,2,1:T(8,128)(2,1)S(1)} %get-tuple-element.479), kind=kOutput, calls=%fused_computation.25.clone.1 | convolution fusion | flops 805699584 | bytes 15728644 | tf_op jit(solution)/shard_map/while/body/eval_jaxpr/hbk,khd->bhd/dot_general | solution.py:411
  398.3 8.5 %bitcast_add_fusion.4 = f32[1024,12,64]{0,2,1:T(8,128)} fusion(f32[1024,12,64]{0,2,1:T(8,128)} %get-tuple-element.463, bf16[12,512,1024]{2,1,0:T(8,128)(2,1)} %multiply_convert_fusion.3, pred[]{:T(512)S(6)} %compare.45, bf16[2,512,12,64]{1,3,2,0:T(8,128)(2,1)S(1)} %get-tuple-element.478, s32[]{:T(128)S(6)} %copy.77), kind=kOutput, calls=%fused_computation.24.clone.1 | convolution fusion | flops 807665664 | bytes 19660804 | tf_op jit(solution)/shard_map/while/body/eval_jaxpr/hbk,bhd->khd/dot_general | solution.py:415
  407.5 10.1 %fusion.133 = f32[12,512,1024]{2,1,0:T(8,128)} fusion(bf16[1024,12,64]{0,2,1:T(8,128)(2,1)S(1)} %get-tuple-element.479, bf16[2,512,12,64]{1,3,2,0:T(8,128)(2,1)S(1)} %get-tuple-element.478, s32[]{:T(128)S(6)} %copy.77), kind=kOutput, calls=%fused_computation.30.clone.1 | convolution fusion | flops 805306368 | bytes 27525124 | tf_op jit(solution)/shard_map/while/body/eval_jaxpr/bhd,khd->hbk/dot_general | solution.py:353
  417.6 13.9 %bitcast_add_fusion.5 = f32[1024,12,64]{0,2,1:T(8,128)} fusion(f32[1024,12,64]{0,2,1:T(8,128)} %get-tuple-element.464, f32[12,512,1024]{2,1,0:T(8,128)} %fusion.133, f32[12,512]{1,0:T(8,128)S(1)} %dynamic-slice_bitcast_fusion.2, pred[1024]{0:T(1024)(128)(4,1)S(1)} %iota_compare_fusion.8, pred[]{:T(512)S(6)} %compare.45, ...), kind=kOutput, calls=%fused_computation.23.clone.1 | convolution fusion | flops 832045056 | bytes 32277508 | tf_op jit(solution)/shard_map/while/body/eval_jaxpr/hbk,bhd->khd/dot_general | solution.py:418
  431.5 17.4 %multiply_reduce_fusion.8 = (f32[12,512]{1,0:T(8,128)S(1)}, f32[12,512,1024]{2,1,0:T(8,128)}) fusion(f32[12,512,1024]{2,1,0:T(8,128)} %fusion.133, f32[12,512]{1,0:T(8,128)S(1)} %dynamic-slice_bitcast_fusion.2, pred[1024]{0:T(1024)(128)(4,1)S(1)} %iota_compare_fusion.8, bf16[1024,12,64]{0,2,1:T(8,128)(2,1)} %get-tuple-element.482, ...), kind=kOutput, calls=%fused_computation.18.clone.1 | convolution fusion | flops 836757504 | bytes 52741124 | tf_op jit(solution)/shard_map/while/body/eval_jaxpr/bhd,khd->hbk/dot_general | solution.py:407
  448.9 21.4 %multiply_convert_fusion.3 = bf16[12,512,1024]{2,1,0:T(8,128)(2,1)} fusion(f32[12,512,1024]{2,1,0:T(8,128)} %get-tuple-element.424, f32[12,512,1024]{2,1,0:T(8,128)} %fusion.133, f32[12,512]{1,0:T(8,128)S(1)} %get-tuple-element.425, f32[12,512]{1,0:T(8,128)S(1)} %dynamic-slice_bitcast_fusion.2, pred[1024]{0:T(1024)(128)(4,1)S(1)} %iota_compare_fusion.8), kind=kLoop, calls=%fused_computation.17.clone.1 | loop fusion | flops 37748736 | bytes 62964736 | tf_op jit(solution)/shard_map/while/body/eval_jaxpr/convert_element_type | solution.py:409
  470.4 9.4 %bitcast_dynamic-update-slice_fusion.8 = bf16[2,512,12,64]{1,3,2,0:T(8,128)(2,1)} fusion(bf16[2,512,12,64]{1,3,2,0:T(8,128)(2,1)} %get-tuple-element.465, s32[]{:T(128)S(6)} %copy.77, bf16[12,512,1024]{2,1,0:T(8,128)(2,1)} %multiply_convert_fusion.3, bf16[1024,12,64]{0,2,1:T(8,128)(2,1)S(1)} %get-tuple-element.479), kind=kOutput, calls=%fused_computation.25.clone.1 | convolution fusion | flops 805699584 | bytes 15728644 | tf_op jit(solution)/shard_map/while/body/eval_jaxpr/hbk,khd->bhd/dot_general | solution.py:411
  479.8 9.4 %bitcast_add_fusion.4 = f32[1024,12,64]{0,2,1:T(8,128)} fusion(f32[1024,12,64]{0,2,1:T(8,128)} %get-tuple-element.463, bf16[12,512,1024]{2,1,0:T(8,128)(2,1)} %multiply_convert_fusion.3, pred[]{:T(512)S(6)} %compare.45, bf16[2,512,12,64]{1,3,2,0:T(8,128)(2,1)S(1)} %get-tuple-element.478, s32[]{:T(128)S(6)} %copy.77), kind=kOutput, calls=%fused_computation.24.clone.1 | convolution fusion | flops 807665664 | bytes 19660804 | tf_op jit(solution)/shard_map/while/body/eval_jaxpr/hbk,bhd->khd/dot_general | solution.py:415
  489.4 3.2 copy.44
  493.3 2.3 convert.59
  498.0 5.5 multiply_add_fusion
  503.5 3.5 copy.50
  509.4 8.5 %fusion.42 = bf16[768,2304]{0,1:T(8,128)(2,1)} fusion(bf16[1024,768]{1,0:T(8,128)(2,1)S(1)} %copy-done.39, bf16[1024,768]{0,1:T(8,128)(2,1)S(1)} %bitcast.213, bf16[1024,768]{0,1:T(8,128)(2,1)S(1)} %bitcast.210, bf16[1024,768]{0,1:T(8,128)(2,1)S(1)} %bitcast.207), kind=kOutput, calls=%fused_computation.69 | convolution fusion | flops 3639803904 | bytes 9830400 | tf_op jit(solution)/shard_map/td,te->de/dot_general | solution.py:435
  517.9 4.3 copy.46
  527.0 2.3 copy-done
  530.6 95.4 %scatter_grads.1 = (f32[432,128]{1,0:T(8,128)S(1)}, f32[144,128]{1,0:T(8,128)S(1)}, f32[576,128]{1,0:T(8,128)S(1)}, f32[576,128]{1,0:T(8,128)S(1)}, f32[16,128]{1,0:T(8,128)S(1)}) custom-call(bf16[4,2,2,2,432,128]{5,4,3,2,1,0:T(8,128)(2,1)S(1)} %bitcast.177, bf16[4,2,2,2,144,128]{5,4,3,2,1,0:T(8,128)(2,1)S(1)} %bitcast.179, ...), custom_call_target="tpu_custom_call" | custom-call | tf_op jit(solution)/shard_map/scatter_grads/pallas_call | solution.py:224
  (216 shorter events, 60.4 us)
Async XLA Ops:
  0.6 7.2 %copy-start.38 = (bf16[1024,768]{1,0:T(8,128)(2,1)S(1)}, bf16[1024,768]{1,0:T(8,128)(2,1)}, u32[]{:S(2)}) copy-start(bf16[1024,768]{1,0:T(8,128)(2,1)} %param.15) | copy-start | bytes 4718596
  5.2 4.3 copy-start.5
  5.2 4.3 copy-start.6
  5.2 4.3 copy-start.7
  5.2 4.3 copy-start.9
  107.6 9.5 %copy-start.13 = (bf16[4,2,2,2,24,2304]{5,4,3,2,1,0:T(8,128)(2,1)S(1)}, bf16[4,2,2,2,24,2304]{5,4,3,2,1,0:T(8,128)(2,1)}, u32[]{:S(2)}) copy-start(bf16[4,2,2,2,24,2304]{5,4,3,2,1,0:T(8,128)(2,1)} %copy-done.12) | copy-start | bytes 10616836
  141.3 11.4 %copy-start.23 = (bf16[1024,12,64]{0,2,1:T(8,128)(2,1)S(1)}, bf16[1024,12,64]{0,2,1:T(8,128)(2,1)}, u32[]{:S(2)}) copy-start(bf16[1024,12,64]{0,2,1:T(8,128)(2,1)} %get-tuple-element.447) | copy-start | bytes 4718596 | tf_op jit(solution)/shard_map/while
  141.3 11.4 %copy-start.35 = (bf16[2,512,12,64]{1,3,2,0:T(8,128)(2,1)S(1)}, bf16[2,512,12,64]{1,3,2,0:T(8,128)(2,1)}, u32[]{:S(2)}) copy-start(bf16[2,512,12,64]{1,3,2,0:T(8,128)(2,1)} %get-tuple-element.435) | copy-start | bytes 4718596 | tf_op jit(solution)/shard_map/while
  175.8 11.4 %copy-start.23 = (bf16[1024,12,64]{0,2,1:T(8,128)(2,1)S(1)}, bf16[1024,12,64]{0,2,1:T(8,128)(2,1)}, u32[]{:S(2)}) copy-start(bf16[1024,12,64]{0,2,1:T(8,128)(2,1)} %get-tuple-element.447) | copy-start | bytes 4718596 | tf_op jit(solution)/shard_map/while
  175.8 11.4 %copy-start.35 = (bf16[2,512,12,64]{1,3,2,0:T(8,128)(2,1)S(1)}, bf16[2,512,12,64]{1,3,2,0:T(8,128)(2,1)}, u32[]{:S(2)}) copy-start(bf16[2,512,12,64]{1,3,2,0:T(8,128)(2,1)} %get-tuple-element.435) | copy-start | bytes 4718596 | tf_op jit(solution)/shard_map/while
  199.8 4.7 copy-start.18
  199.8 4.7 copy-start.21
  199.8 4.7 copy-start.16
  199.8 4.7 copy-start.37
  199.8 4.7 copy-start.56
  204.5 2.9 slice-start
  204.5 3.4 slice-start.1
  204.5 44.1 %slice-start.4 = ((s8[4718592]{0:T(1024)(128)(4,1)}), s8[4194304]{0:T(1024)(128)(4,1)S(1)}, s32[]{:S(2)}) async-start(s8[4718592]{0:T(1024)(128)(4,1)} %bitcast.193), calls=%async_computation.4 | async-start | bytes 8388608
  206.2 42.4 %copy-start.31 = (f32[1024,768]{0,1:T(8,128)}, f32[1024,768]{0,1:T(8,128)S(1)}, u32[]{:S(2)}) copy-start(f32[1024,768]{0,1:T(8,128)S(1)} %get-tuple-element.302) | copy-start | bytes 9437188
  206.6 41.9 %copy-start.46 = (f32[1024]{0:T(1024)}, f32[1024]{0:T(1024)S(1)}, u32[]{:S(2)}) copy-start(f32[1024]{0:T(1024)S(1)} %multiply_reduce_fusion.6) | copy-start | bytes 12292
  208.9 39.7 %slice-start.5 = ((s8[4718592]{0:T(1024)(128)(4,1)}), s8[524288]{0:T(1024)(128)(4,1)S(1)}, s32[]{:S(2)}) async-start(s8[4718592]{0:T(1024)(128)(4,1)} %bitcast.193), calls=%async_computation.5 | async-start | bytes 1048576
  208.9 39.7 %copy-start.55 = (f32[768]{0:T(1024)S(1)}, f32[768]{0:T(1024)}, u32[]{:S(2)}) copy-start(f32[768]{0:T(1024)} %get-tuple-element.241) | copy-start | bytes 9220
  248.5 6.0 copy-start.58
  248.6 5.9 copy-start.26
  248.6 5.9 copy-start.43
  248.6 5.9 copy-start.44
  254.5 4.8 copy-start.24
  261.9 32.8 %slice-start.2 = ((s8[4718592]{0:T(1024)(128)(4,1)}), s8[4194304]{0:T(1024)(128)(4,1)S(1)}, s32[]{:S(2)}) async-start(s8[4718592]{0:T(1024)(128)(4,1)} %bitcast.189), calls=%async_computation.2 | async-start | bytes 8388608
  266.4 28.3 %slice-start.3 = ((s8[4718592]{0:T(1024)(128)(4,1)}), s8[524288]{0:T(1024)(128)(4,1)S(1)}, s32[]{:S(2)}) async-start(s8[4718592]{0:T(1024)(128)(4,1)} %bitcast.189), calls=%async_computation.3 | async-start | bytes 1048576
  285.0 9.7 %copy-start.25 = (f32[1024,768]{0,1:T(8,128)S(1)}, f32[1024,768]{0,1:T(8,128)}, u32[]{:S(2)}) copy-start(f32[1024,768]{0,1:T(8,128)} %copy-done.24) | copy-start | bytes 9437188
  285.0 9.7 %copy-start.32 = (f32[1024,768]{0,1:T(8,128)S(1)}, f32[1024,768]{0,1:T(8,128)}, u32[]{:S(2)}) copy-start(f32[1024,768]{0,1:T(8,128)} %copy-done.31) | copy-start | bytes 9437188
  285.0 9.7 %copy-start.57 = (bf16[1024,3072]{1,0:T(8,128)(2,1)S(1)}, bf16[1024,3072]{1,0:T(8,128)(2,1)}, u32[]{:S(2)}) copy-start(bf16[1024,3072]{1,0:T(8,128)(2,1)} %get-tuple-element.308) | copy-start | bytes 18874372
  294.7 7.0 %copy-start.47 = (f32[1024]{0:T(1024)S(1)}, f32[1024]{0:T(1024)}, u32[]{:S(2)}) copy-start(f32[1024]{0:T(1024)} %copy-done.46) | copy-start | bytes 12292
  302.5 10.1 %copy-start.29 = (f32[1024,768]{0,1:T(8,128)}, f32[1024,768]{0,1:T(8,128)S(1)}, u32[]{:S(2)}) copy-start(f32[1024,768]{0,1:T(8,128)S(1)} %get-tuple-element.286) | copy-start | bytes 9437188
  309.7 6.7 %copy-start.50 = (f32[1024]{0:T(1024)}, f32[1024]{0:T(1024)S(1)}, u32[]{:S(2)}) copy-start(f32[1024]{0:T(1024)S(1)} %negate_multiply_fusion.1) | copy-start | bytes 12292
  314.0 3.1 copy-start.17
  321.7 4.4 copy-start.19
  321.7 4.4 copy-start.22
  321.7 4.4 copy-start.42
  327.0 10.1 %copy-start.28 = (bf16[2,512,12,64]{1,3,2,0:T(8,128)(2,1)S(1)}, bf16[2,512,12,64]{1,3,2,0:T(8,128)(2,1)}, u32[]{:S(2)}) copy-start(bf16[2,512,12,64]{1,3,2,0:T(8,128)(2,1)} %get-tuple-element.481) | copy-start | bytes 4718596 | tf_op jit(solution)/shard_map/while
  407.5 10.1 %copy-start.28 = (bf16[2,512,12,64]{1,3,2,0:T(8,128)(2,1)S(1)}, bf16[2,512,12,64]{1,3,2,0:T(8,128)(2,1)}, u32[]{:S(2)}) copy-start(bf16[2,512,12,64]{1,3,2,0:T(8,128)(2,1)} %get-tuple-element.481) | copy-start | bytes 4718596 | tf_op jit(solution)/shard_map/while
  489.4 3.6 copy-start.20
  493.0 3.7 copy-start.27
  493.0 3.7 copy-start.30
  493.3 4.7 copy-start.14
  493.3 4.7 copy-start.45
  493.3 4.7 copy-start.51
  517.9 5.5 copy-start.53
  (21 other events, 33.4 us)

commit v2 on v1

v2 whole, which is shorter than its diff:
```python
import functools

import jax
import jax.numpy as jnp
from jax import lax
from jax.experimental import pallas as pl
from jax.experimental.pallas import tpu as pltpu
from jax.sharding import PartitionSpec as P

MESH = pl.DeviceIdType.MESH
GRID = (4, 2, 2, 2)
LANES = 128
ANY = pl.BlockSpec(memory_space=pl.ANY)
VMEM = pl.BlockSpec(memory_space=pltpu.VMEM)


def place():
    me = lax.axis_index("dp")
    return me // 8, (me // 4) % 2, (me // 2) % 2, me % 2


def device(z, y, x, c):
    return ((z * 2 + y) * 2 + x) * 2 + c


def remote(src, dst, send, recv, to):
    return pltpu.make_async_remote_copy(
        src_ref=src, dst_ref=dst, send_sem=send, recv_sem=recv, device_id=(to,), device_id_type=MESH
    )


def meet(z, y, x, c):
    barrier = pltpu.get_barrier_semaphore()
    others = [device((z + k) % 4, y, x, c) for k in (1, 2, 3)]
    others += [device(z, 1 - y, x, c), device(z, y, 1 - x, c), device(z, y, x, 1 - c)]
    for other in others:
        pl.semaphore_signal(barrier, inc=1, device_id=(other,), device_id_type=MESH)
    pl.semaphore_wait(barrier, len(others))


def gather_kernel(count, *refs):
    shards, outs = refs[:count], refs[count : 2 * count]
    send, recv, local = refs[2 * count :]
    z, y, x, c = place()
    meet(z, y, x, c)
    y_to, x_to, c_to = device(z, 1 - y, x, c), device(z, y, 1 - x, c), device(z, y, x, 1 - c)
    low, high = pl.ds(0, 2), pl.ds(2, 2)
    every, both = pl.ds(0, 4), pl.ds(0, 2)
    arrays = range(count)

    def copy(w, slot, where, to):
        return remote(outs[w].at[where], outs[w].at[where], send.at[w, slot], recv.at[w, slot], to)

    pending = []

    def go(w, slot, where, to):
        one = copy(w, slot, where, to)
        one.start()
        pending.append(one)

    def arrived(w, slot, where):
        copy(w, slot, where, c_to).wait_recv()

    own = [pltpu.make_async_copy(shards[w], outs[w].at[z, y, x, c], local.at[w]) for w in arrays]
    for w in arrays:
        own[w].start()
        for k in (1, 2, 3):
            one = remote(
                shards[w],
                outs[w].at[z, y, x, c],
                send.at[w, k - 1],
                recv.at[w, k - 1],
                device((z + k) % 4, y, x, c),
            )
            one.start()
            pending.append(one)
    for w in arrays:
        own[w].wait()
        for k in (1, 2, 3):
            arrived(w, k - 1, ((z + 4 - k) % 4, y, x, c))
        go(w, 3, (low, y, x, c), x_to)
        go(w, 4, (high, y, x, c), y_to)
        go(w, 7, (every, y, x, c), c_to)
    for w in arrays:
        arrived(w, 3, (low, y, 1 - x, c))
        go(w, 5, (low, y, both, c), y_to)
        go(w, 8, (low, y, 1 - x, c), c_to)
        arrived(w, 4, (high, 1 - y, x, c))
        go(w, 6, (high, both, x, c), x_to)
        go(w, 9, (high, 1 - y, x, c), c_to)
    for w in arrays:
        arrived(w, 5, (low, 1 - y, both, c))
        go(w, 10, (low, 1 - y, both, c), c_to)
        arrived(w, 6, (high, both, 1 - x, c))
        go(w, 11, (high, both, 1 - x, c), c_to)
    for w in arrays:
        arrived(w, 7, (every, y, x, 1 - c))
        arrived(w, 8, (low, y, 1 - x, 1 - c))
        arrived(w, 9, (high, 1 - y, x, 1 - c))
        arrived(w, 10, (low, 1 - y, both, 1 - c))
        arrived(w, 11, (high, both, 1 - x, 1 - c))
    for one in pending:
        one.wait_send()


def gather(shards):
    count = len(shards)
    return pl.pallas_call(
        functools.partial(gather_kernel, count),
        out_shape=[jax.ShapeDtypeStruct(GRID + s.shape, s.dtype) for s in shards],
        in_specs=[VMEM] * count,
        out_specs=[ANY] * count,
        scratch_shapes=[
            pltpu.SemaphoreType.DMA((count, 12)),
            pltpu.SemaphoreType.DMA((count, 12)),
            pltpu.SemaphoreType.DMA((count,)),
        ],
        compiler_params=pltpu.CompilerParams(
            collective_id=0, has_side_effects=True, vmem_limit_bytes=8 << 20
        ),
        name="gather_weights",
    )(*shards)


def scatter_kernel(count, *refs):
    grads, sums = refs[:count], refs[count : 2 * count]
    groups = [refs[2 * count + 7 * w : 2 * count + 7 * (w + 1)] for w in range(count)]
    send, recv, local = refs[9 * count :]
    z, y, x, c = place()
    meet(z, y, x, c)
    y_to, x_to, c_to = device(z, 1 - y, x, c), device(z, y, 1 - x, c), device(z, y, x, 1 - c)
    low, high = pl.ds(0, 2), pl.ds(2, 2)
    every, both = pl.ds(0, 4), pl.ds(0, 2)
    arrays = range(count)
    f32 = jnp.float32
    pending = []

    def go(src, dst, w, slot, to):
        one = remote(src, dst, send.at[w, slot], recv.at[w, slot], to)
        one.start()
        pending.append(one)
        return one

    def add(dst, src, total):
        def step(i, carry):
            a, b = dst(i), src(i)
            a[...] = (a[...].astype(f32) + b[...].astype(f32)).astype(a.dtype)
            return carry

        lax.fori_loop(0, total, step, 0)

    own, first = [], []
    for w in arrays:
        acc, r0 = groups[w][:2]
        first.append(go(grads[w].at[every, both, both, 1 - c], r0, w, 0, c_to))
        one = pltpu.make_async_copy(grads[w].at[every, both, both, c], acc, local.at[w])
        one.start()
        own.append(one)
    second = []
    for w in arrays:
        acc, r0, r1a, r1b, r2a, r2b, r3 = groups[w]
        own[w].wait()
        first[w].wait_recv()
        add(
            lambda i: acc.at[i // 4, (i // 2) % 2, i % 2],
            lambda i: r0.at[i // 4, (i // 2) % 2, i % 2],
            16,
        )
        second.append(
            (
                go(acc.at[low, both, 1 - x], r1a, w, 1, x_to),
                go(acc.at[high, 1 - y, both], r1b, w, 2, y_to),
            )
        )
    third = []
    for w in arrays:
        acc, r0, r1a, r1b, r2a, r2b, r3 = groups[w]
        second[w][0].wait_recv()
        add(lambda i: acc.at[i // 2, i % 2, x], lambda i: r1a.at[i // 2, i % 2], 4)
        a = go(acc.at[low, 1 - y, x], r2a, w, 3, y_to)
        second[w][1].wait_recv()
        add(lambda i: acc.at[2 + i // 2, y, i % 2], lambda i: r1b.at[i // 2, i % 2], 4)
        b = go(acc.at[high, y, 1 - x], r2b, w, 4, x_to)
        third.append((a, b))
    last = []
    for w in arrays:
        acc, r0, r1a, r1b, r2a, r2b, r3 = groups[w]
        third[w][0].wait_recv()
        add(lambda i: acc.at[i, y, x], lambda i: r2a.at[i], 2)
        third[w][1].wait_recv()
        add(lambda i: acc.at[2 + i, y, x], lambda i: r2b.at[i], 2)
        last.append(
            [
                go(
                    acc.at[(z + k) % 4, y, x],
                    r3.at[k - 1],
                    w,
                    4 + k,
                    device((z + k) % 4, y, x, c),
                )
                for k in (1, 2, 3)
            ]
        )
    for w in arrays:
        acc, r0, r1a, r1b, r2a, r2b, r3 = groups[w]
        for one in last[w]:
            one.wait_recv()
        sums[w][...] = (
            (acc[z, y, x].astype(f32) + r3[0].astype(f32))
            + (r3[1].astype(f32) + r3[2].astype(f32))
        )
    for one in pending:
        one.wait_send()


def scatter(grads):
    count = len(grads)
    scratch = []
    for g in grads:
        rows = g.shape[4]
        bf16 = g.dtype
        for shape in ((4, 2, 2), (4, 2, 2), (2, 2), (2, 2), (2,), (2,), (3,)):
            scratch.append(pltpu.VMEM(shape + (rows, LANES), bf16))
    return pl.pallas_call(
        functools.partial(scatter_kernel, count),
        out_shape=[jax.ShapeDtypeStruct(g.shape[4:], jnp.float32) for g in grads],
        in_specs=[ANY] * count,
        out_specs=[VMEM] * count,
        scratch_shapes=scratch
        + [
            pltpu.SemaphoreType.DMA((count, 8)),
            pltpu.SemaphoreType.DMA((count, 8)),
            pltpu.SemaphoreType.DMA((count,)),
        ],
        compiler_params=pltpu.CompilerParams(
            collective_id=1, has_side_effects=True, vmem_limit_bytes=40 << 20
        ),
        name="scatter_grads",
    )(*grads)


def as_slabs(grad):
    rows, cols = grad.shape[0] // 32, grad.shape[1]
    tiles = grad.reshape(32, rows // 8, 8, cols // LANES, LANES).transpose(0, 1, 3, 2, 4)
    return tiles.reshape(GRID + (rows * cols // LANES, LANES))


def from_slab(slab, rows, cols):
    tiles = slab.reshape(rows // 8, cols // LANES, 8, LANES).transpose(0, 2, 1, 3)
    return tiles.reshape(rows, cols)

H = 12
EPSILON = 1e-05

LOG2E = 1.4426950408889634
DEAD = -1e30


def exact_parts(value):
    low = jnp.bfloat16
    f32 = jnp.float32
    one = value.astype(low)
    rest = value - one.astype(f32)
    two = rest.astype(low)
    three = (rest - two.astype(f32)).astype(low)
    return one, two, three


def attend_kernel(head_dim, block, length_ref, q_ref, k_ref, v_ref, o_ref, lse_ref, qq, kk, vv):
    f32, bf16 = jnp.float32, jnp.bfloat16
    seq, width = q_ref.shape
    lane = lax.broadcasted_iota(jnp.int32, (1, width), 1)
    row = lax.broadcasted_iota(jnp.int32, (seq, 1), 0)
    first = lane < head_dim
    q = q_ref[...].astype(f32) * (head_dim**-0.5 * LOG2E)
    q_high = q.astype(bf16).astype(f32)
    q_low = q - q_high
    k, v = k_ref[...].astype(f32), v_ref[...].astype(f32)
    dead = jnp.where(row < length_ref[0], 0.0, DEAD)
    for h in (0, 1):
        data = first if h == 0 else lane >= head_dim
        spot = head_dim * (1 - h)
        qq[h, :, :width] = jnp.where(data, q_high, jnp.where(lane == spot, 1.0, 0.0)).astype(bf16)
        qq[h, :, width:] = jnp.where(data, q_low, 0.0).astype(bf16)
        kk[h, :, :width] = jnp.where(data, k, jnp.where(lane == spot, dead, 0.0)).astype(bf16)
        kk[h, :, width:] = k_ref[...]
        vv[h] = jnp.where(data, v, 1.0).astype(bf16)

    def one_block(i, carry):
        at = pl.ds(pl.multiple_of(i * block, block), block)
        outs, tops = [], []
        for h in (0, 1):
            s = lax.dot_general(
                qq[h, at], kk[h], (((1,), (1,)), ((), ())), preferred_element_type=f32
            )
            top = jnp.max(s, axis=1, keepdims=True)
            p = jnp.exp2(s - top).astype(bf16)
            outs.append(jnp.dot(p, vv[h], preferred_element_type=f32))
            tops.append(top)
        mixed = jnp.where(first, outs[0], outs[1])
        sums = jnp.where(first, outs[1], outs[0])
        o_ref[at, :] = (mixed / pltpu.roll(sums, head_dim, 1)).astype(bf16)
        lse_ref[at, :] = jnp.where(first, tops[1], tops[0]) + jnp.log2(sums)
        return carry

    lax.fori_loop(0, seq // block, one_block, 0)


def attend(length, proj, heads, block=512):
    seq, width = proj.shape[0], proj.shape[1] // 3
    pairs, head_dim = heads // 2, width // heads
    two = 2 * head_dim

    def part(n):
        return pl.BlockSpec((seq, two), lambda p: (0, n * pairs + p))

    out = pl.BlockSpec((seq, two), lambda p: (0, p))
    return pl.pallas_call(
        functools.partial(attend_kernel, head_dim, block),
        grid=(pairs,),
        out_shape=[
            jax.ShapeDtypeStruct((seq, width), jnp.bfloat16),
            jax.ShapeDtypeStruct((seq, width), jnp.float32),
        ],
        in_specs=[pl.BlockSpec(memory_space=pltpu.SMEM), part(0), part(1), part(2)],
        out_specs=[out, out],
        scratch_shapes=[
            pltpu.VMEM((2, seq, 2 * two), jnp.bfloat16),
            pltpu.VMEM((2, seq, 2 * two), jnp.bfloat16),
            pltpu.VMEM((2, seq, two), jnp.bfloat16),
        ],
        compiler_params=pltpu.CompilerParams(vmem_limit_bytes=48 << 20),
        name="attend_fwd",
    )(length, proj, proj, proj)


def attend_back_kernel(
    head_dim, block, length_ref, q_ref, k_ref, v_ref, do_ref, o_ref, lse_ref,
    dq_ref, dk_ref, dv_ref, qq, kk, vv, dd, dk_acc, dv_acc, kt,
):
    f32, bf16 = jnp.float32, jnp.bfloat16
    seq, width = q_ref.shape
    scale = head_dim**-0.5
    lane = lax.broadcasted_iota(jnp.int32, (1, width), 1)
    row = lax.broadcasted_iota(jnp.int32, (seq, 1), 0)
    first = lane < head_dim
    q = q_ref[...].astype(f32) * (scale * LOG2E)
    q_high = q.astype(bf16).astype(f32)
    q_low = q - q_high
    k, v, do = k_ref[...].astype(f32), v_ref[...].astype(f32), do_ref[...].astype(f32)
    dead = jnp.where(row < length_ref[0], 0.0, DEAD)
    swap_r = lax.broadcasted_iota(jnp.int32, (width, width), 0) < head_dim
    swap_c = lax.broadcasted_iota(jnp.int32, (width, width), 1) < head_dim
    swap = jnp.where(swap_r != swap_c, 1.0, 0.0).astype(bf16)
    terms = exact_parts(do * o_ref[...].astype(f32))
    delta = sum(jnp.dot(t, swap, preferred_element_type=f32) for t in terms)
    l_parts = [t.astype(f32) for t in exact_parts(-lse_ref[...])]
    d_parts = [t.astype(f32) for t in exact_parts(-delta)]
    kt[...] = k.T.astype(bf16)
    for h in (0, 1):
        data = first if h == 0 else lane >= head_dim
        spot = head_dim * (1 - h)

        def place(spots):
            value = 0.0
            for n, part in spots:
                value = jnp.where(lane == spot + n, part, value)
            return value

        qx = place([(0, 1.0)] + [(1 + n, l_parts[n]) for n in range(3)])
        kx = place([(0, dead)] + [(1 + n, 1.0) for n in range(3)])
        dx = place([(n, d_parts[n]) for n in range(3)])
        vx = place([(n, 1.0) for n in range(3)])
        qq[h, :, :width] = jnp.where(data, q_high, qx).astype(bf16)
        qq[h, :, width:] = jnp.where(data, q_low, 0.0).astype(bf16)
        kk[h, :, :width] = jnp.where(data, k, kx).astype(bf16)
        kk[h, :, width:] = k_ref[...]
        vv[h] = jnp.where(data, v, vx).astype(bf16)
        dd[h] = jnp.where(data, do, dx).astype(bf16)
    dk_acc[...] = jnp.zeros_like(dk_acc)
    dv_acc[...] = jnp.zeros_like(dv_acc)
    across = (((1,), (1,)), ((), ()))

    def one_block(i, carry):
        at = pl.ds(pl.multiple_of(i * block, block), block)
        turned = []
        for h in (0, 1):
            p = jnp.exp2(lax.dot_general(kk[h], qq[h, at], across, preferred_element_type=f32))
            dp = lax.dot_general(vv[h], dd[h, at], across, preferred_element_type=f32)
            ds = (p * dp).astype(bf16)
            dv_acc[h] += jnp.dot(p.astype(bf16), do_ref[at, :], preferred_element_type=f32)
            dk_acc[h] += jnp.dot(ds, q_ref[at, :], preferred_element_type=f32)
            turned.append(
                jnp.dot(
                    kt[pl.ds(h * head_dim, head_dim), :], ds, preferred_element_type=f32
                )
            )
        dq = jnp.concatenate(turned, axis=0).T
        dq_ref[at, :] = (dq * scale).astype(bf16)
        return carry

    lax.fori_loop(0, seq // block, one_block, 0)
    dk_ref[...] = (jnp.where(first, dk_acc[0], dk_acc[1]) * scale).astype(bf16)
    dv_ref[...] = jnp.where(first, dv_acc[0], dv_acc[1]).astype(bf16)


def attend_back(length, proj, d_heads, heads_out, lse, heads, block=512):
    seq, width = proj.shape[0], proj.shape[1] // 3
    pairs, head_dim = heads // 2, width // heads
    two = 2 * head_dim

    def part(n):
        return pl.BlockSpec((seq, two), lambda p: (0, n * pairs + p))

    one = pl.BlockSpec((seq, two), lambda p: (0, p))
    return pl.pallas_call(
        functools.partial(attend_back_kernel, head_dim, block),
        grid=(pairs,),
        out_shape=[jax.ShapeDtypeStruct((seq, width), jnp.bfloat16)] * 3,
        in_specs=[pl.BlockSpec(memory_space=pltpu.SMEM), part(0), part(1), part(2), one, one, one],
        out_specs=[one] * 3,
        scratch_shapes=[
            pltpu.VMEM((2, seq, 2 * two), jnp.bfloat16),
            pltpu.VMEM((2, seq, 2 * two), jnp.bfloat16),
            pltpu.VMEM((2, seq, two), jnp.bfloat16),
            pltpu.VMEM((2, seq, two), jnp.bfloat16),
            pltpu.VMEM((2, seq, two), jnp.float32),
            pltpu.VMEM((2, seq, two), jnp.float32),
            pltpu.VMEM((two, seq), jnp.bfloat16),
        ],
        compiler_params=pltpu.CompilerParams(vmem_limit_bytes=56 << 20),
        name="attend_bwd",
    )(length, proj, proj, proj, d_heads, heads_out, lse)

def erf_of(x):
    x = jnp.clip(x, -3.7439211627767994, 3.7439211627767994)
    s = x * x
    top = 0.00022905065861350646
    for c in (0.0034082910107109506, 0.050955695062380861, 0.18520832239976145, 1.128379143519084):
        top = top * s + c
    low = -1.1791602954361697e-7
    for c in (
        0.000023547966471313185,
        0.0010179625278914885,
        0.014070470171167667,
        0.11098505178285362,
        0.49746925110067538,
        1.0,
    ):
        low = low * s + c
    return x * top / low


def centre(h):
    shifted = h - jnp.mean(h, axis=1, keepdims=True)
    scale = lax.rsqrt(jnp.mean(shifted * shifted, axis=1, keepdims=True) + EPSILON)
    return shifted * scale, scale


def centre_back(dy, gain, hat, scale):
    d = dy * gain
    return scale * (
        d - jnp.mean(d, axis=1, keepdims=True) - hat * jnp.mean(d * hat, axis=1, keepdims=True)
    )


def middle_kernel(
    chunk, length_ref, drop_ref, x_ref, cot_ref, o_ref, w_out, w_up, w_down, vec, b_up,
    result_ref, dh1_ref, do_ref, act_ref, du_ref, x1_ref, df_ref, da_ref, dvec, db_up, slope,
):
    f32, bf16 = jnp.float32, jnp.bfloat16
    rows = x_ref.shape[0]
    hidden = w_up.shape[1]
    step = pl.program_id(0)
    row = step * rows + lax.broadcasted_iota(jnp.int32, (rows, 1), 0)
    live = jnp.where(row < length_ref[0], 1.0, 0.0)
    keep = (1 - drop_ref[0]).astype(f32)
    b_out, g1, s1, b_down, g2, s2 = [vec[n : n + 1, :] for n in range(2, 8)]
    across = (((1,), (1,)), ((), ()))

    @pl.when(step == 0)
    def _():
        dvec[...] = jnp.zeros_like(dvec)
        db_up[...] = jnp.zeros_like(db_up)

    x = x_ref[...].astype(f32)
    h1 = x + (jnp.dot(o_ref[...], w_out[...], preferred_element_type=f32) + b_out)
    hat1, scale1 = centre(h1)
    x1 = hat1 * g1 + s1
    x1_low = x1.astype(bf16)
    x1_ref[...] = x1_low
    ff = b_down
    for n in range(0, hidden, chunk):
        at = slice(n, n + chunk)
        u = jnp.dot(x1_low, w_up[:, at], preferred_element_type=f32) + b_up[:, at]
        upper = 0.5 + 0.5 * erf_of(u * 0.7071067811865476)
        slope[:, at] = upper + u * (0.3989422804014327 * jnp.exp(-0.5 * (u * u)))
        act = (u * upper).astype(bf16)
        act_ref[:, at] = act
        ff = ff + jnp.dot(act, w_down[at, :], preferred_element_type=f32)
    h2 = x1 + ff
    hat2, scale2 = centre(h2)
    result_ref[...] = (live * (keep * (hat2 * g2 + s2) + (1 - keep) * x)).astype(bf16)
    dy = (keep * live) * cot_ref[...].astype(f32)
    dh2 = centre_back(dy, g2, hat2, scale2)
    df = dh2.astype(bf16)
    df_ref[...] = df
    dvec[5:6, :] += jnp.sum(df.astype(f32), axis=0, keepdims=True)
    dvec[6:7, :] += jnp.sum(dy * hat2, axis=0, keepdims=True)
    dvec[7:8, :] += jnp.sum(dy, axis=0, keepdims=True)
    dx1 = dh2
    for n in range(0, hidden, chunk):
        at = slice(n, n + chunk)
        da_ff = lax.dot_general(df, w_down[at, :], across, preferred_element_type=f32)
        du = (da_ff * slope[:, at]).astype(bf16)
        du_ref[:, at] = du
        db_up[:, at] += jnp.sum(du.astype(f32), axis=0, keepdims=True)
        dx1 = dx1 + lax.dot_general(du, w_up[:, at], across, preferred_element_type=f32)
    dvec[3:4, :] += jnp.sum(dx1 * hat1, axis=0, keepdims=True)
    dvec[4:5, :] += jnp.sum(dx1, axis=0, keepdims=True)
    dh1 = centre_back(dx1, g1, hat1, scale1)
    dh1_ref[...] = dh1
    da = dh1.astype(bf16)
    da_ref[...] = da
    dvec[2:3, :] += jnp.sum(da.astype(f32), axis=0, keepdims=True)
    do_ref[...] = lax.dot_general(da, w_out[...], across, preferred_element_type=f32).astype(bf16)


def middle(length, drop, tokens, cotangent, heads_out, w_out, w_up, w_down, vec, b_up, block=256, chunk=768):
    seq, width = tokens.shape
    hidden = w_up.shape[1]
    f32, bf16 = jnp.float32, jnp.bfloat16
    smem = pl.BlockSpec(memory_space=pltpu.SMEM)
    thin = pl.BlockSpec((block, width), lambda i: (i, 0))
    wide = pl.BlockSpec((block, hidden), lambda i: (i, 0))

    def whole(shape):
        return pl.BlockSpec(shape, lambda i: (0, 0), pipeline_mode=pl.Buffered(1))

    def like(cols, dtype):
        return jax.ShapeDtypeStruct((seq, cols), dtype)

    return pl.pallas_call(
        functools.partial(middle_kernel, chunk),
        grid=(seq // block,),
        out_shape=[
            like(width, bf16),
            like(width, f32),
            like(width, bf16),
            like(hidden, bf16),
            like(hidden, bf16),
            like(width, bf16),
            like(width, bf16),
            like(width, bf16),
            jax.ShapeDtypeStruct((8, width), f32),
            jax.ShapeDtypeStruct((1, hidden), f32),
        ],
        in_specs=[smem, smem, thin, thin, thin]
        + [whole(w.shape) for w in (w_out, w_up, w_down, vec, b_up)],
        out_specs=[thin, thin, thin, wide, wide, thin, thin, thin]
        + [pl.BlockSpec(s, lambda i: (0, 0)) for s in ((8, width), (1, hidden))],
        scratch_shapes=[
            pltpu.VMEM((block, hidden), f32),
        ],
        compiler_params=pltpu.CompilerParams(vmem_limit_bytes=60 << 20),
        name="middle",
    )(length, drop, tokens, cotangent, heads_out, w_out, w_up, w_down, vec, b_up)

def tail_kernel(
    length_ref, drop_ref, dq_ref, dk_ref, dv_ref, dh1_ref, cot_ref, w_ref, out_ref, sums
):
    f32 = jnp.float32
    rows, width = dh1_ref.shape
    step = pl.program_id(0)
    row = step * rows + lax.broadcasted_iota(jnp.int32, (rows, 1), 0)
    live = jnp.where(row < length_ref[0], 1.0, 0.0)
    keep = (1 - drop_ref[0]).astype(f32)
    across = (((1,), (1,)), ((), ()))

    @pl.when(step == 0)
    def _():
        sums[...] = jnp.zeros_like(sums)

    total = dh1_ref[...]
    for n, part in enumerate((dq_ref, dk_ref, dv_ref)):
        total = total + lax.dot_general(
            part[...], w_ref[:, n * width : (n + 1) * width], across, preferred_element_type=f32
        )
    out_ref[...] = keep * total + ((1 - keep) * live) * cot_ref[...].astype(f32)
    sums[0:1, :] += jnp.sum(dq_ref[...].astype(f32), axis=0, keepdims=True)
    sums[1:2, :] += jnp.sum(dv_ref[...].astype(f32), axis=0, keepdims=True)


def tail(length, drop, dq, dk, dv, dh1, cotangent, w_qkv, block=256):
    seq, width = dq.shape
    smem = pl.BlockSpec(memory_space=pltpu.SMEM)
    thin = pl.BlockSpec((block, width), lambda i: (i, 0))
    weight = pl.BlockSpec(w_qkv.shape, lambda i: (0, 0), pipeline_mode=pl.Buffered(1))
    return pl.pallas_call(
        tail_kernel,
        grid=(seq // block,),
        out_shape=[
            jax.ShapeDtypeStruct((seq, width), jnp.float32),
            jax.ShapeDtypeStruct((8, width), jnp.float32),
        ],
        in_specs=[smem, smem, thin, thin, thin, thin, thin, weight],
        out_specs=[thin, pl.BlockSpec((8, width), lambda i: (0, 0))],
        compiler_params=pltpu.CompilerParams(vmem_limit_bytes=40 << 20),
        name="grad_tokens",
    )(length, drop, dq, dk, dv, dh1, cotangent, w_qkv)

def pack(attn_vectors, ffn_vectors, up_bias):
    rows = jnp.concatenate([attn_vectors.T, ffn_vectors.T], axis=0).reshape(-1)
    return jnp.concatenate([rows, up_bias])


def unpack(shares, rows):
    devices = shares.shape[0]
    vec = shares[:, : 8 * rows].reshape(devices, 8, rows).transpose(1, 0, 2)
    hidden = shares[:, 8 * rows : 12 * rows].reshape(1, -1)
    return vec.reshape(8, -1).astype(jnp.float32), hidden.astype(jnp.float32)


def repack(d_vec, d_hidden, devices):
    rows = d_vec.shape[1] // devices
    vec = d_vec.reshape(8, devices, rows).transpose(1, 0, 2).reshape(devices, -1)
    return jnp.concatenate([vec, d_hidden.reshape(devices, -1)], axis=1)


def fetch_plain(w_qkv, w_out, w_up, w_down, small):
    weights = tuple(
        lax.all_gather(w, "dp", axis=0, tiled=True) for w in (w_qkv, w_out, w_up, w_down)
    )
    return (*weights, lax.all_gather(small, "dp", axis=0))


def spread_plain(grads, small):
    f32 = jnp.float32
    sums = [lax.psum_scatter(g.astype(f32), "dp", scatter_dimension=0, tiled=True) for g in grads]
    return sums, lax.psum_scatter(small, "dp", scatter_dimension=0)


def fetch_kernel(w_qkv, w_out, w_up, w_down, small):
    share = small.shape[0]
    small = jnp.pad(small, (0, 16 * LANES - share)).reshape(16, LANES)
    full = gather([w_qkv, w_out, w_up, w_down, small])
    weights = tuple(f.reshape(-1, f.shape[-1]) for f in full[:4])
    return (*weights, full[4].reshape(-1, 16 * LANES)[:, :share])


def spread_kernel(grads, small):
    devices, share = small.shape
    small = jnp.pad(small, ((0, 0), (0, 16 * LANES - share))).astype(jnp.bfloat16)
    sums = scatter([as_slabs(g) for g in grads] + [small.reshape(GRID + (16, LANES))])
    back = [from_slab(s, g.shape[0] // devices, g.shape[1]) for s, g in zip(sums, grads)]
    return back, sums[-1].reshape(-1)[:share]


def transposed(left, right):
    return jnp.einsum("ta,tb->ab", left, right, preferred_element_type=jnp.float32).astype(
        jnp.bfloat16
    )


def local(
    fetch,
    spread,
    tokens,
    lengths,
    drops,
    cotangent,
    w_qkv,
    w_out,
    w_up,
    w_down,
    attn_vectors,
    ffn_vectors,
    up_bias,
):
    f32, bf16 = jnp.float32, jnp.bfloat16
    rows = w_qkv.shape[0]
    width = tokens.shape[1]
    qkv_full, out_full, up_full, down_full, shares = fetch(
        w_qkv, w_out, w_up, w_down, pack(attn_vectors, ffn_vectors, up_bias)
    )
    vec, b_up = unpack(shares, rows)
    qkv_bias = jnp.concatenate([vec[0], jnp.zeros((width,), f32), vec[1]])
    proj = (jnp.dot(tokens, qkv_full, preferred_element_type=f32) + qkv_bias).astype(bf16)
    heads_out, log_sums = attend(lengths, proj, H)
    result, dh1, d_heads, act, d_pre, x1, d_ff, d_attn, d_vec, d_up_bias = middle(
        lengths, drops, tokens, cotangent, heads_out, out_full, up_full, down_full, vec, b_up
    )
    dq, dk, dv = attend_back(lengths, proj, d_heads, heads_out, log_sums, H)
    grad_tokens, proj_sums = tail(lengths, drops, dq, dk, dv, dh1, cotangent, qkv_full)
    grads = [transposed(tokens, d) for d in (dq, dk, dv)]
    grads += [transposed(heads_out, d_attn), transposed(x1, d_pre), transposed(act, d_ff)]
    small = repack(d_vec + proj_sums, d_up_bias, lax.axis_size("dp"))
    sums, small = spread(grads, small)
    d_vec, d_up_bias = small[: 8 * rows].reshape(8, rows), small[8 * rows :]
    return (
        result,
        grad_tokens,
        jnp.concatenate(sums[:3], axis=1),
        sums[3],
        sums[4],
        sums[5],
        d_vec[:5].T,
        d_vec[5:].T,
        d_up_bias,
    )


def solution(mesh):
    kernels = mesh.shape["dp"] == 32
    layer = functools.partial(
        local, fetch_kernel if kernels else fetch_plain, spread_kernel if kernels else spread_plain
    )
    rows, line = P("dp", None), P("dp")
    return jax.shard_map(
        layer,
        mesh=mesh,
        in_specs=(rows, line, line, rows, rows, rows, rows, rows, rows, rows, line),
        out_specs=(rows, rows, rows, rows, rows, rows, rows, rows, line),
        check_vma=False,
    )
```

time: 647 us -> 396 us (0.61); the launches traced: 638 us -> 395 us
  matrix products: 275 us -> 33 us
  Pallas kernels: 186 us -> 313 us
  other arithmetic: 88.5 us -> 6.44 us
  local copies, waits for them, and re-layouts: 84.1 us -> 40.6 us
    dot_general x25 -> x6, matrix products: 269 us -> 25.7 us  [transposed(): jnp.einsum('ta,tb->ab', left, right, preferred_element_type=jnp.float32)]
    pallas_call x0 -> x4, Pallas kernels: none -> 131 us  [the longest x1 49.5 us: attend_back(): pl.pallas_call(functools.partial(attend_back_kernel, head_dim, block), gr...]
    convert_element_type x6 -> x2, other arithmetic: 44.8 us -> 0.69 us  [unpack(): return (vec.reshape(8, -1).astype(jnp.float32), hidden.astype(jnp.float32))]
    reduce_sum x9 -> x0, other arithmetic: 35.6 us -> none  [the longest x2 22.8 us: attend(): totals = jnp.sum(expo, axis=-1, keepdims=True)]
    unnamed x140 -> x51, local copies, waits for them, and re-layouts: 45.1 us -> 21.7 us
    another operation x14 -> x0, local copies, waits for them, and re-layouts: 10.5 us -> none
    convert_element_type x6 -> x7, local copies, waits for them, and re-layouts: 13.2 us -> 8.53 us  [the longest x4 5.41 us: unpack(): return (vec.reshape(8, -1).astype(jnp.float32), hidden.astype(jnp.float32))]
where the time goes in v2:
time: 396 us; the launch traced here: 395 us
  Pallas kernels  313 us (79%)
  local copies, waits for them, and re-layouts  40.6 us (10%)
  matrix products  33 us (8%)
  other arithmetic  6.44 us (2%)
    pallas_call x1, Pallas kernels, gather(): pl.pallas_call(functools.partial(gather_kernel, count), out_shape=[jax.Sh...  90.9 us
    pallas_call x1, Pallas kernels, scatter(): pl.pallas_call(functools.partial(scatter_kernel, count), out_shape=[jax.S...  90.6 us
    pallas_call x1, Pallas kernels, attend_back(): pl.pallas_call(functools.partial(attend_back_kernel, head_dim, block), gr...  49.5 us
    pallas_call x1, Pallas kernels, middle(): pl.pallas_call(functools.partial(middle_kernel, chunk), grid=(seq // bloc...  47 us
    pallas_call x1, Pallas kernels, attend(): pl.pallas_call(functools.partial(attend_kernel, head_dim, block), grid=(p...  29 us
    dot_general x6, matrix products, transposed(): jnp.einsum('ta,tb->ab', left, right, preferred_element_type=jnp.float32)  25.7 us
    unnamed x51, local copies, waits for them, and re-layouts  21.7 us

profile of v2, /device:TPU:0, one launch (start us, length us, event | category | flops | bytes accessed | tf_op | source)
XLA Modules:
  0.0 395.1 jit_solution(10910276068673300041)
XLA Ops:
  1.9 0.7 pad_maximum_fusion.2
  2.7 0.7 fusion.11.refs_4_
  3.5 0.9 copy-done.14
  4.4 0.9 copy-done.15
  5.3 0.9 copy-done.16
  6.2 0.8 copy-done.18
  7.0 90.9 %gather_weights.1 = (bf16[4,2,2,2,24,2304]{5,4,3,2,1,0:T(8,128)(2,1)S(1)}, bf16[4,2,2,2,24,768]{5,4,3,2,1,0:T(8,128)(2,1)S(1)}, bf16[4,2,2,2,24,3072]{5,4,3,2,1,...) custom-call(bf16[24,2304]{1,0:T(8,128)(2,1)S(1)} %copy-done.16, ...), custom_call_target="tpu_custom_call" | custom-call | tf_op jit(solution)/shard_map/gather_weights/pallas_call | solution.py:108
  97.8 2.1 copy-done.3
  100.0 2.2 copy-done.4
  102.2 1.0 copy-done.11
  104.6 1.5 reshape.198
  106.1 1.7 slice_reduce_fusion.1
  107.8 1.6 copy.27
  109.4 1.6 convert_element_type.56.vec
  111.0 1.4 squeeze.6
  113.1 0.7 pad_maximum_fusion.1
  113.8 7.3 %fusion.q_ref.k_ref.v_ref = bf16[1024,2304]{1,0:T(8,128)(2,1)} fusion(bf16[1024,768]{1,0:T(8,128)(2,1)} %x_ref.1, bf16[768,2304]{1,0:T(8,128)(2,1)S(1)} %bitcast.110, f32[2304]{0:T(1024)S(1)} %pad_maximum_fusion.1), kind=kOutput, calls=%fused_computation.3 | convolution fusion | flops 3628597248 | bytes 9839616 | tf_op jit(solution)/shard_map/dot_general | solution.py:688
  121.1 29.0 %attend_fwd.1 = (bf16[1024,768]{1,0:T(8,128)(2,1)S(1)}, f32[1024,768]{1,0:T(8,128)S(1)}) custom-call(s32[1]{0:T(128)S(6)} %copy.40.length_ref, bf16[1024,2304]{1,0:T(8,128)(2,1)} %fusion.q_ref.k_ref.v_ref, bf16[1024,2304]{1,0:T(8,128)(2,1)} %fusion.q_ref.k_ref.v_ref, bf16[1024,2304]{1,0:T(8,128)(2,1)} %fusion.q_ref.k_ref.v_ref), custom_call_target="tpu_custom_call" | custom-call | tf_op jit(solution)/shard_map/attend_fwd/pallas_call | solution.py:318
  150.2 1.1 copy-done.1
  151.3 1.7 copy-done.6
  153.1 47.0 %middle.1 = (bf16[1024,768]{1,0:T(8,128)(2,1)}, f32[1024,768]{1,0:T(8,128)}, bf16[1024,768]{1,0:T(8,128)(2,1)}, bf16[1024,3072]{1,0:T(8,128)(2,1)}, bf16[1024,30...) custom-call(s32[1]{0:T(128)S(6)} %copy.40.length_ref, ...), custom_call_target="tpu_custom_call" | custom-call | tf_op jit(solution)/shard_map/middle/pallas_call | solution.py:543
  200.1 49.5 %attend_bwd.1 = (bf16[1024,768]{1,0:T(8,128)(2,1)}, bf16[1024,768]{1,0:T(8,128)(2,1)}, bf16[1024,768]{1,0:T(8,128)(2,1)}) custom-call(s32[1]{0:T(128)S(6)} %copy.40.length_ref, bf16[1024,2304]{1,0:T(8,128)(2,1)} %fusion.q_ref.k_ref.v_ref, bf16[1024,2304]{1,0:T(8,128)(2,1)} %fusion.q_ref.k_ref.v_ref, bf16[1024,2304]{1,0:T(8,128)(2,1)} %fusion.q_ref.k_ref.v_ref, ...), custom_call_target="tpu_custom_call" | custom-call | tf_op jit(solution)/shard_map/attend_bwd/pallas_call | solution.py:416
  249.6 2.5 convolution_convert_fusion.2
  252.1 0.7 copy-done.7
  252.9 1.4 copy-done.8
  254.3 1.4 copy-done.9
  255.7 6.0 %grad_tokens.1 = (f32[1024,768]{1,0:T(8,128)}, f32[8,768]{1,0:T(8,128)S(1)}) custom-call(s32[1]{0:T(128)S(6)} %copy.40.length_ref, s32[1]{0:T(128)S(6)} %copy.41.drop_ref, bf16[1024,768]{1,0:T(8,128)(2,1)S(1)} %copy-done.7, bf16[1024,768]{1,0:T(8,128)(2,1)S(1)} %copy-done.8, bf16[1024,768]{1,0:T(8,128)(2,1)S(1)} %copy-done.9, f32[1024,768]{1,0:T(8,128)S(1)} %copy-done.5, ...), custom_call_target="tpu_custom_call" | custom-call | tf_op jit(solution)/shard_map/grad_tokens/pallas_call | solution.py:599
  261.7 2.5 fusion.3
  264.1 1.4 fusion.2
  265.6 1.4 fusion.1
  267.7 0.9 copy.29
  268.6 1.6 copy.30
  270.2 0.8 add_convert_fusion.1
  270.9 1.3 convert_reduce_fusion
  272.3 1.4 reshape.182
  273.7 0.8 reshape.180
  274.4 1.5 copy.31
  275.9 1.0 reshape.181
  276.9 0.8 fusion.7
  277.7 7.8 %convolution_convert_fusion.1 = bf16[768,3072]{1,0:T(8,128)(2,1)S(1)} fusion(bf16[1024,768]{1,0:T(8,128)(2,1)} %get-tuple-element.53, bf16[1024,3072]{1,0:T(8,128)(2,1)} %get-tuple-element.54), kind=kOutput, calls=%fused_computation.2 | convolution fusion | flops 4834197504 | bytes 12582912 | tf_op jit(solution)/shard_map/ta,tb->ab/dot_general | solution.py:660
  285.5 10.0 %convolution_convert_fusion = bf16[3072,768]{1,0:T(8,128)(2,1)} fusion(bf16[1024,3072]{1,0:T(8,128)(2,1)} %get-tuple-element.55, bf16[1024,768]{1,0:T(8,128)(2,1)S(1)} %copy-done.21), kind=kOutput, calls=%fused_computation.1 | convolution fusion | flops 4834197504 | bytes 12582912 | tf_op jit(solution)/shard_map/ta,tb->ab/dot_general | solution.py:660
  295.5 90.6 %scatter_grads.1 = (f32[144,128]{1,0:T(8,128)S(1)}, f32[144,128]{1,0:T(8,128)S(1)}, f32[144,128]{1,0:T(8,128)S(1)}, f32[144,128]{1,0:T(8,128)S(1)}, f32[576,128]...) custom-call(bf16[4,2,2,2,144,128]{5,4,3,2,1,0:T(8,128)(2,1)S(1)} %bitcast.104, ...), custom_call_target="tpu_custom_call" | custom-call | tf_op jit(solution)/shard_map/scatter_grads/pallas_call | solution.py:224
  386.1 0.7 copy-done.12
  386.8 0.7 copy-done.13
  387.5 0.7 pad_maximum_fusion
  390.2 1.5 copy.42
  391.7 1.7 copy.43
  393.4 1.7 copy.44
  (46 shorter events, 4.9 us)
Async XLA Ops:
  3.5 0.9 copy-start.14
  4.4 0.9 copy-start.15
  5.3 0.9 copy-start.16
  6.2 0.8 copy-start.18
  97.8 2.2 copy-start.3
  100.0 2.2 copy-start.4
  102.2 1.0 copy-start.11
  150.2 1.2 copy-start.1
  151.3 1.7 copy-start.6
  200.1 49.5 %copy-start.2 = (bf16[1024,768]{1,0:T(8,128)(2,1)S(1)}, bf16[1024,768]{1,0:T(8,128)(2,1)}, u32[]{:S(2)}) copy-start(bf16[1024,768]{1,0:T(8,128)(2,1)} %copy-done.1) | copy-start | bytes 4718596
  200.1 49.5 %copy-start.22 = (bf16[1024,768]{1,0:T(8,128)(2,1)S(1)}, bf16[1024,768]{1,0:T(8,128)(2,1)}, u32[]{:S(2)}) copy-start(bf16[1024,768]{1,0:T(8,128)(2,1)} %get-tuple-element.52) | copy-start | bytes 4718596
  249.6 2.5 copy-start
  249.6 2.5 copy-start.5
  249.6 3.2 copy-start.7
  252.9 1.4 copy-start.8
  254.3 1.4 copy-start.9
  255.7 6.0 %copy-start.20 = (bf16[1024,768]{1,0:T(8,128)(2,1)S(1)}, bf16[1024,768]{1,0:T(8,128)(2,1)}, u32[]{:S(2)}) copy-start(bf16[1024,768]{1,0:T(8,128)(2,1)} %x_ref.1) | copy-start | bytes 4718596
  261.7 2.5 copy-start.19
  277.7 7.8 %copy-start.21 = (bf16[1024,768]{1,0:T(8,128)(2,1)S(1)}, bf16[1024,768]{1,0:T(8,128)(2,1)}, u32[]{:S(2)}) copy-start(bf16[1024,768]{1,0:T(8,128)(2,1)} %get-tuple-element.56) | copy-start | bytes 4718596
  285.5 10.0 %copy-start.10 = (bf16[768,768]{1,0:T(8,128)(2,1)S(1)}, bf16[768,768]{1,0:T(8,128)(2,1)}, u32[]{:S(2)}) copy-start(bf16[768,768]{1,0:T(8,128)(2,1)} %convolution_convert_fusion.2) | copy-start | bytes 3538948
  386.1 0.7 copy-start.12
  386.8 0.7 copy-start.13
  387.5 0.7 copy-start.17
